TPU v7x, 32 devices: a whole 2x2x4 slice. The times are simulated.
32 devices in a mesh: groups: 2 (over y), dp: 4 (over z), kv: 4 (over x, core).
Axes of the slice: x: 2, y: 2, z: 4, core: 2. Of those that a mesh axis runs over, the one named last changes fastest.
Arguments:
- queries: bfloat16 [128, 3, 8192], P(('groups', 'dp'), None, 'kv'), parts along dimension 0, may hold values from -12 to 12
- routes: int32 [128, 1], P(('groups', 'dp')), parts along dimension 0, may hold values from 0 to 3; in each aligned block of 16 rows (0 to 15, 16 to 31, ...) at most 8 rows name the same one
- suffix_lengths: int32 [128], P(('groups', 'dp')), parts along dimension 0, may hold values from 128 to 256
- prefix_keys: bfloat16 [8, 2048, 1024], P(('groups', 'dp'), None, 'kv'), parts along dimension 0, may hold values from -8 to 8
- prefix_values: bfloat16 [8, 2048, 1024], P(('groups', 'dp'), None, 'kv'), parts along dimension 0, may hold values from -4.5 to 4.5
- suffix_keys: bfloat16 [128, 256, 1024], P(('groups', 'dp'), None, 'kv'), parts along dimension 0, may hold values from -4.5 to 4.5
- suffix_values: bfloat16 [128, 256, 1024], P(('groups', 'dp'), None, 'kv'), parts along dimension 0, may hold values from -4.5 to 4.5
- new_keys: bfloat16 [128, 3, 1024], P(('groups', 'dp'), None, 'kv'), parts along dimension 0, may hold values from -4.5 to 4.5
- new_values: bfloat16 [128, 3, 1024], P(('groups', 'dp'), None, 'kv'), parts along dimension 0, may hold values from -4.5 to 4.5
- out_weight: bfloat16 [8192, 8192], P('kv', 'dp'), may hold values from -0.0625 to 0.0625
Outputs:
- projected: bfloat16 [128, 3, 8192], P(('groups', 'kv'), None, 'dp'), parts along dimension 0
There are 2 independent parts, one for each index of `groups`. A program takes and returns all parts, laid end to end along the dimension named above; an argument that names none is the same for every part. Nothing has to cross between parts.
Inputs may be any that keep to these rules, and one draw needn't show every extreme that they name: `routes`: among the 16 candidates of one index of dp at most 8 continue the same prompt, and in every draw some prompt receives exactly 8 of them from some index.
All inputs are finite; a program needn't handle non-finite values.
Results may differ from a plain program's by a relative error of at most 0.008.
Values may be sent and summed in bfloat16 or wider, within the bound.
No kernel may reach another device: no remote copies, remote signals or barrier semaphores. Data moves between devices by JAX's collectives and lax.ppermute only.
A program may use at most 128 MiB of HBM per device.

v0:
```python
import math

import jax
import jax.numpy as jnp
from jax import lax
from jax.sharding import PartitionSpec as P

HD = 128


def local(
    queries,
    routes,
    suffix_lengths,
    prefix_keys,
    prefix_values,
    suffix_keys,
    suffix_values,
    new_keys,
    new_values,
    out_weight,
):
    owners_count = lax.axis_size("dp")
    cand_count, step_count, query_width = queries.shape
    kv_width = prefix_keys.shape[2]
    kv_heads = kv_width // HD
    group_size = query_width // kv_width
    capacity = max(2, 2 * cand_count // owners_count)
    score_scale = 1.0 / math.sqrt(HD)
    owner_index = routes[:, 0]
    owner_table = (
        owner_index[:, None] == jnp.arange(owners_count, dtype=jnp.int32)[None, :]
    ).astype(jnp.int32)
    earlier_same = jnp.cumsum(owner_table, 0) - owner_table
    slot_rank = jnp.sum(earlier_same * owner_table, 1)
    slot_index = owner_index * capacity + slot_rank
    placement = (
        slot_index[None, :] == jnp.arange(owners_count * capacity, dtype=jnp.int32)[:, None]
    ).astype(jnp.bfloat16)
    outgoing = jnp.dot(
        placement,
        queries.reshape(cand_count, step_count * query_width),
        preferred_element_type=jnp.float32,
    )
    outgoing = outgoing.astype(jnp.bfloat16).reshape(
        owners_count, capacity, step_count, query_width
    )
    prompt_keys = prefix_keys[0].reshape(-1, kv_heads, HD)
    prompt_values = prefix_values[0].reshape(-1, kv_heads, HD).astype(jnp.float32)
    received = lax.all_to_all(outgoing, "dp", split_axis=0, concat_axis=0, tiled=True)
    row_shape = received.shape
    query_heads = received.reshape(-1, kv_heads, group_size, HD)
    scores = (
        jnp.einsum("rhgd,khd->rhgk", query_heads, prompt_keys, preferred_element_type=jnp.float32)
        * score_scale
    )
    peak_score = jnp.max(scores, -1, keepdims=True)
    weights = jnp.exp(scores - peak_score)
    weight_sum = jnp.sum(weights, -1, keepdims=True)
    combined = jnp.einsum("rhgk,khd->rhgd", weights, prompt_values) / weight_sum
    log_total = (peak_score + jnp.log(weight_sum))[..., 0]
    homeward = (
        lax.all_to_all(combined.reshape(row_shape), "dp", split_axis=0, concat_axis=0, tiled=True),
        lax.all_to_all(
            log_total.reshape(row_shape[0], row_shape[1], row_shape[2], kv_heads * group_size),
            "dp",
            split_axis=0,
            concat_axis=0,
            tiled=True,
        ),
    )
    prompt_rows = homeward[0]
    prompt_totals = homeward[1]
    prompt_rows = jnp.take(
        prompt_rows.reshape(owners_count * capacity, step_count, query_width), slot_index, axis=0
    )
    prompt_totals = jnp.take(
        prompt_totals.reshape(owners_count * capacity, step_count, kv_heads * group_size),
        slot_index,
        axis=0,
    )
    query_heads = queries.reshape(cand_count, step_count, kv_heads, group_size, HD)
    cache_keys = suffix_keys.reshape(cand_count, -1, kv_heads, HD)
    cache_length = cache_keys.shape[1]
    cache_scores = jnp.einsum(
        "cshgd,cjhd->cshgj", query_heads, cache_keys, preferred_element_type=jnp.float32
    )
    fresh_scores = jnp.einsum(
        "cshgd,cthd->cshgt",
        query_heads,
        new_keys.reshape(cand_count, step_count, kv_heads, HD),
        preferred_element_type=jnp.float32,
    )
    scores = jnp.concatenate([cache_scores, fresh_scores], -1) * score_scale
    cache_allowed = jnp.arange(cache_length, dtype=jnp.int32)[None, :] < suffix_lengths[:, None]
    step_positions = jnp.arange(step_count, dtype=jnp.int32)
    fresh_allowed = step_positions[None, :] <= step_positions[:, None]
    allowed = jnp.concatenate(
        [
            jnp.broadcast_to(cache_allowed[:, None, :], (cand_count, step_count, cache_length)),
            jnp.broadcast_to(fresh_allowed[None, :, :], (cand_count, step_count, step_count)),
        ],
        -1,
    )
    scores = jnp.where(allowed[:, :, None, None, :], scores, -jnp.inf)
    peak_score = jnp.max(scores, -1, keepdims=True)
    weights = jnp.exp(scores - peak_score)
    weight_sum = jnp.sum(weights, -1, keepdims=True)
    value_rows = jnp.concatenate(
        [
            suffix_values.reshape(cand_count, -1, kv_heads, HD),
            new_values.reshape(cand_count, step_count, kv_heads, HD),
        ],
        1,
    ).astype(jnp.float32)
    suffix_rows = jnp.einsum("cshgj,cjhd->cshgd", weights, value_rows) / weight_sum
    suffix_totals = (peak_score + jnp.log(weight_sum))[..., 0]
    prompt_rows = prompt_rows.reshape(cand_count, step_count, kv_heads, group_size, HD)
    prompt_totals = prompt_totals.reshape(cand_count, step_count, kv_heads, group_size)
    common_peak = jnp.maximum(prompt_totals, suffix_totals)
    prompt_share = jnp.exp(prompt_totals - common_peak)[..., None]
    suffix_share = jnp.exp(suffix_totals - common_peak)[..., None]
    attended = (prompt_share * prompt_rows + suffix_share * suffix_rows) / (
        prompt_share + suffix_share
    )
    attended = attended.reshape(cand_count, step_count, query_width).astype(jnp.bfloat16)
    block_rows = lax.all_gather(attended, "dp", axis=0, tiled=True)
    row_count = block_rows.shape[0]
    product = jnp.dot(
        block_rows.reshape(-1, query_width), out_weight, preferred_element_type=jnp.float32
    )
    partial_value = product.reshape(row_count, step_count, -1)
    return lax.psum_scatter(partial_value, "kv", scatter_dimension=0, tiled=True).astype(
        jnp.bfloat16
    )


def solution(mesh):
    placed = (
        P(("groups", "dp"), None, "kv"),
        P(("groups", "dp"), None),
        P(("groups", "dp")),
        P(("groups", "dp"), None, "kv"),
        P(("groups", "dp"), None, "kv"),
        P(("groups", "dp"), None, "kv"),
        P(("groups", "dp"), None, "kv"),
        P(("groups", "dp"), None, "kv"),
        P(("groups", "dp"), None, "kv"),
        P("kv", "dp"),
    )
    return jax.shard_map(
        local,
        mesh=mesh,
        in_specs=placed,
        out_specs=P(("groups", "kv"), None, "dp"),
        check_vma=False,
    )
```

profile of v0, /device:TPU:0, one launch (start us, length us, event | category | flops | bytes accessed | tf_op | source)
XLA Modules:
  0.0 142.7 jit_solution(114557513929737650)
XLA Ops:
  6.5 0.8 fusion.46
  7.4 0.8 select_reduce_fusion
  8.2 0.7 multiply_add_fusion
  8.9 0.9 copy.132
  9.8 1.0 convolution_convert_fusion
  10.8 6.3 %all-to-all-start = ((bf16[4,8,3,2048]{3,1,2,0:T(8,128)(2,1)}), bf16[4,8,3,2048]{3,1,2,0:T(8,128)(2,1)S(1)}, u32[]{:S(2)}, u32[]{:S(2)}) async-start(bf16[4,8,3,2048]{3,1,2,0:T(8,128)(2,1)} %bitcast.3), calls=%async_computation | async-start | bytes 786432 | tf_op jit(solution)/shard_map/all_to_all | solution.py:50
  17.2 0.3 reshape_squeeze.7
  17.5 1.3 reshape_squeeze.8
  18.9 0.1 iota_compare_fusion
  19.0 0.6 pad_add_fusion
  19.6 9.2 %all-to-all-done = bf16[4,8,3,2048]{3,1,2,0:T(8,128)(2,1)S(1)} async-done(((bf16[4,8,3,2048]{3,1,2,0:T(8,128)(2,1)}), bf16[4,8,3,2048]{3,1,2,0:T(8,128)(2,1)S(1)}, u32[]{:S(2)}, u32[]{:S(2)}) %all-to-all-start) | async-done | bytes 393248 | tf_op jit(solution)/shard_map/all_to_all | solution.py:50
  28.8 0.3 copy.91
  29.2 0.5 reshape.137
  29.7 6.4 %bitcast_reduce_fusion = (f32[96,2,8]{2,0,1:T(8,128)S(1)}, f32[2,96,8,2048]{3,2,1,0:T(8,128)}) fusion(bf16[2048,2,128,1]{2,1,0,3:T(2,128)(2,1)S(1)} %bitcast.96, bf16[96,2,8,128]{3,2,1,0:T(8,128)(2,1)S(1)} %reshape.137), kind=kOutput, calls=%fused_computation.3 | convolution fusion | flops 811596288 | bytes 14030848 | tf_op jit(solution)/shard_map/rhgd,khd->rhgk/dot_general | solution.py:54
  36.1 6.1 %fusion.3 = f32[96,2,8]{2,0,1:T(8,128)S(1)} fusion(f32[2,96,8,2048]{3,2,1,0:T(8,128)} %get-tuple-element.11, f32[96,2,8]{2,0,1:T(8,128)S(1)} %get-tuple-element.10), kind=kLoop, calls=%fused_computation.6 | loop fusion | flops 9435648 | bytes 12595200 | tf_op jit(solution)/shard_map/reduce_sum | solution.py:59
  42.2 0.1 copy.94
  42.3 0.1 copy.96
  42.5 0.1 add.61
  42.6 0.7 reshape.169
  43.3 3.2 %all-to-all-start.1 = ((f32[4,1,384]{2,1,0:T(1,128)}), f32[4,1,384]{2,1,0:T(1,128)S(1)}, u32[]{:S(2)}, u32[]{:S(2)}) async-start(f32[4,1,384]{2,1,0:T(1,128)} %reshape.169), calls=%async_computation.1 | async-start | bytes 12288 | tf_op jit(solution)/shard_map/all_to_all | solution.py:64
  46.5 5.7 %fusion.30 = f32[96,2,8,128]{3,2,0,1:T(8,128)S(1)} fusion(bf16[2048,2,128,1]{2,1,0,3:T(2,128)(2,1)S(1)} %bitcast.99, f32[2,96,8,2048]{3,2,1,0:T(8,128)} %get-tuple-element.11, f32[96,2,8]{2,0,1:T(8,128)S(1)} %get-tuple-element.10, f32[96,2,8]{2,0,1:T(8,128)S(1)} %fusion.3), kind=kOutput, calls=%fused_computation.34 | convolution fusion | flops 811794432 | bytes 14430208 | tf_op jit(solution)/shard_map/rhgk,khd->rhgd/dot_general | solution.py:60
  52.3 0.3 reshape.142
  52.7 1.3 copy.108
  54.0 5.0 %all-to-all-start.2 = ((f32[4,8,3,2048]{3,1,2,0:T(8,128)}), f32[4,8,3,2048]{3,1,2,0:T(8,128)S(1)}, u32[]{:S(2)}, u32[]{:S(2)}) async-start(f32[4,8,3,2048]{3,1,2,0:T(8,128)} %copy.108), calls=%async_computation.2 | async-start | bytes 1572864 | tf_op jit(solution)/shard_map/all_to_all | solution.py:63
  59.1 2.1 %reshape.139 = bf16[16,256,2,128]{3,2,1,0:T(2,128)(2,1)} reshape(bf16[16,256,256]{2,1,0:T(8,128)(2,1)S(1)} %copy-done) | data formatting | bytes 4194304 | tf_op jit(solution)/shard_map/reshape | solution.py:83
  61.2 2.9 %copy.112 = bf16[16,256,256]{1,2,0:T(8,128)(2,1)S(1)} copy(bf16[16,256,256]{2,1,0:T(8,128)(2,1)} %param.16) | data formatting | bytes 4194304 | tf_op args[6]
  64.1 2.4 %copy.113 = bf16[16,256,2,128]{3,1,2,0:T(8,128)(2,1)} copy(bf16[16,256,2,128]{1,3,2,0:T(8,128)(2,1)S(1)} %bitcast.95) | data formatting | bytes 4194304 | tf_op jit(solution)/shard_map/reshape | solution.py:111
  66.5 0.2 convolution_bitcast_fusion
  66.8 2.2 %fusion.16 = f32[16,3,2,8,256]{4,3,1,2,0:T(8,128)S(1)} fusion(bf16[16,256,2,128,1]{3,2,1,0,4:T(2,128)(2,1)} %bitcast.98, bf16[16,3,2,8,128]{4,3,2,0,1:T(8,128)(2,1)S(1)} %bitcast.101), kind=kOutput, calls=%fused_computation.19 | convolution fusion | flops 50331648 | bytes 3080192 | tf_op jit(solution)/shard_map/cshgd,cjhd->cshgj/dot_general | solution.py:85
  69.0 0.3 fusion.37
  69.3 0.5 fusion.29
  69.8 0.5 broadcast.96
  70.3 0.7 reduce
  71.0 0.1 reshape.170
  71.1 0.6 gather_fusion
  71.7 0.1 copy.99
  71.8 0.1 copy.100
  71.9 0.7 fusion.51
  72.7 5.5 %all-to-all-done.2 = f32[4,8,3,2048]{3,1,2,0:T(8,128)S(1)} async-done(((f32[4,8,3,2048]{3,1,2,0:T(8,128)}), f32[4,8,3,2048]{3,1,2,0:T(8,128)S(1)}, u32[]{:S(2)}, u32[]{:S(2)}) %all-to-all-start.2) | async-done | bytes 786464 | tf_op jit(solution)/shard_map/all_to_all | solution.py:63
  78.2 0.5 copy.109
  78.7 0.9 gather_fusion.1
  79.6 0.3 reshape.168
  79.9 2.3 %fusion.28 = bf16[16,3,2,8,128]{4,3,1,2,0:T(8,128)(2,1)S(1)} fusion(bf16[16,3,2,128]{3,1,2,0:T(4,128)(2,1)S(1)} %copy.114, bf16[16,256,2,128]{3,1,2,0:T(8,128)(2,1)} %copy.113, f32[16,3,2,8]{3,1,2,0:T(4,128)S(1)} %fusion.37, f32[16,3,2,8,3]{4,3,1,2,0:T(8,128)S(1)} %convolution_bitcast_fusion, f32[16,3,2,8,256]{4,3,1,2,0:T(8,128)S(1)} %fusion.16, ...), kind=kOutput, calls=%fused_computation.32 | convolution fusion | flops 56648704 | bytes 3535008 | tf_op jit(solution)/shard_map/cshgj,cjhd->cshgd/dot_general | solution.py:116
  82.2 0.1 convert_element_type.21
  82.3 17.7 %all_gather.3 = bf16[64,3,2048]{2,0,1:T(8,128)(2,1)S(1)} all-gather(bf16[16,3,2048]{2,0,1:T(8,128)(2,1)S(1)} %convert_element_type.21), channel_id=1, replica_groups=mesh['groups'=2,'dp'=4,'kv'=4] {'dp'}, dimensions={0}, use_global_device_ids=true | all-gather | bytes 983040 | tf_op jit(solution)/shard_map/all_gather | solution.py:127
  100.0 6.4 %fusion.4 = f32[64,3,2048]{2,0,1:T(8,128)} fusion(bf16[64,3,2048]{2,0,1:T(8,128)(2,1)S(1)} %all_gather.3, bf16[2048,2048]{1,0:T(8,128)(2,1)} %param.19), kind=kOutput, calls=%fused_computation.7 | convolution fusion | flops 1610612736 | bytes 10747904 | tf_op jit(solution)/shard_map/dot_general | solution.py:129
  106.4 27.8 %reduce-scatter.2.cloned.1.call-done = f32[16,3,2048]{2,0,1:T(8,128)} async-done(((f32[64,3,2048]{2,0,1:T(8,128)}), f32[16,3,2048]{2,0,1:T(8,128)}) %reduce-scatter.2.cloned.1.call-update) | async-done | bytes 393232 | tf_op jit(solution)/shard_map/reduce_scatter | solution.py:133
  134.2 1.7 %convert_element_type.22 = bf16[16,3,2048]{2,0,1:T(8,128)(2,1)} convert(f32[16,3,2048]{2,0,1:T(8,128)} %reduce-scatter.2.cloned.1.call-done) | non-fusion elementwise | flops 98304 | bytes 589824 | tf_op jit(solution)/shard_map/convert_element_type | solution.py:133
  (35 shorter events, 0.4 us)
Async XLA Ops:
  6.5 10.6 %copy-start.1 = (bf16[1,2048,256]{2,1,0:T(8,128)(2,1)S(1)}, bf16[1,2048,256]{2,1,0:T(8,128)(2,1)}, u32[]{:S(2)}) copy-start(bf16[1,2048,256]{2,1,0:T(8,128)(2,1)} %param.13) | copy-start | bytes 3145732
  10.8 18.0 %all-to-all-start = ((bf16[4,8,3,2048]{3,1,2,0:T(8,128)(2,1)}), bf16[4,8,3,2048]{3,1,2,0:T(8,128)(2,1)S(1)}, u32[]{:S(2)}, u32[]{:S(2)}) async-start(bf16[4,8,3,2048]{3,1,2,0:T(8,128)(2,1)} %bitcast.3), calls=%async_computation | async-start | bytes 786432 | tf_op jit(solution)/shard_map/all_to_all | solution.py:50
  17.2 1.7 %copy-start.7 = (s32[16]{0:T(128)S(1)}, s32[16]{0:T(128)}, u32[]{:S(2)}) copy-start(s32[16]{0:T(128)} %param.12) | copy-start | bytes 196
  17.2 2.4 %copy-start.6 = (s32[16,1]{0,1:T(1,128)S(1)}, s32[16,1]{0,1:T(1,128)}, u32[]{:S(2)}) copy-start(s32[16,1]{0,1:T(1,128)} %param.11) | copy-start | bytes 196
  43.3 10.7 %all-to-all-start.1 = ((f32[4,1,384]{2,1,0:T(1,128)}), f32[4,1,384]{2,1,0:T(1,128)S(1)}, u32[]{:S(2)}, u32[]{:S(2)}) async-start(f32[4,1,384]{2,1,0:T(1,128)} %reshape.169), calls=%async_computation.1 | async-start | bytes 12288 | tf_op jit(solution)/shard_map/all_to_all | solution.py:64
  52.6 6.4 %copy-start.2 = (bf16[16,3,2048]{2,0,1:T(8,128)(2,1)S(1)}, bf16[16,3,2048]{2,0,1:T(8,128)(2,1)}, u32[]{:S(2)}) copy-start(bf16[16,3,2048]{2,0,1:T(8,128)(2,1)} %param.10) | copy-start | bytes 589828
  52.7 6.5 %copy-start = (bf16[16,256,256]{2,1,0:T(8,128)(2,1)S(1)}, bf16[16,256,256]{2,1,0:T(8,128)(2,1)}, u32[]{:S(2)}) copy-start(bf16[16,256,256]{2,1,0:T(8,128)(2,1)} %param.15) | copy-start | bytes 6291460
  54.0 24.2 %all-to-all-start.2 = ((f32[4,8,3,2048]{3,1,2,0:T(8,128)}), f32[4,8,3,2048]{3,1,2,0:T(8,128)S(1)}, u32[]{:S(2)}, u32[]{:S(2)}) async-start(f32[4,8,3,2048]{3,1,2,0:T(8,128)} %copy.108), calls=%async_computation.2 | async-start | bytes 1572864 | tf_op jit(solution)/shard_map/all_to_all | solution.py:63
  59.1 75.1 %reduce-scatter.2.cloned.1.call-start = ((), (), s32[]{:S(2)}) async-start(), calls=%async_computation.4 | async-start | bytes 1966080 | tf_op jit(solution)/shard_map/reduce_scatter | solution.py:133
  59.1 2.1 %copy-start.4 = (bf16[16,3,256]{2,0,1:T(8,128)(2,1)S(1)}, bf16[16,3,256]{2,0,1:T(8,128)(2,1)}, u32[]{:S(2)}) copy-start(bf16[16,3,256]{2,0,1:T(8,128)(2,1)} %param.17) | copy-start | bytes 73732
  64.1 2.4 %copy-start.5 = (bf16[16,3,256]{2,0,1:T(8,128)(2,1)S(1)}, bf16[16,3,256]{2,0,1:T(8,128)(2,1)}, u32[]{:S(2)}) copy-start(bf16[16,3,256]{2,0,1:T(8,128)(2,1)} %param.18) | copy-start | bytes 73732
  66.5 2.5 %copy-start.3 = (pred[16,3,259]{2,1,0:T(4,128)(4,1)S(1)}, pred[16,3,259]{2,1,0:T(4,128)(4,1)}, u32[]{:S(2)}) copy-start(pred[16,3,259]{2,1,0:T(4,128)(4,1)} %pad_add_fusion) | copy-start | bytes 37300
Sparse Core Ops, SparseCore 0:
  106.5 27.5 reduce-scatter.1
where the time goes:
time: 143 us
  waiting for transfers between devices  42.5 us (30%)
  matrix products  24.2 us (17%)
  blocking collectives  17.7 us (12%)
  local copies, waits for them, and re-layouts  16.8 us (12%)
  starting transfers between devices  14.6 us (10%)
  between operations  13.7 us (10%)
  other arithmetic  13.2 us (9%)
    reduce_scatter x1, waiting for transfers between devices, local(): lax.psum_scatter(partial_value, 'kv', scatter_dimension=0, tiled=True)  27.8 us
    all_gather x1, blocking collectives, local(): block_rows = lax.all_gather(attended, 'dp', axis=0, tiled=True)  17.7 us
    all_to_all x1, waiting for transfers between devices, local(): lax.all_to_all(outgoing, 'dp', split_axis=0, concat_axis=0, tiled=True)  9.21 us
    reduce_sum x2, other arithmetic, local(): weight_sum = jnp.sum(weights, -1, keepdims=True)  6.66 us
    dot_general x1, matrix products, local(): jnp.einsum('rhgd,khd->rhgk', query_heads, prompt_keys, preferred_element_...  6.38 us
    dot_general x1, matrix products, local(): jnp.dot(block_rows.reshape(-1, query_width), out_weight, preferred_elemen...  6.36 us
    all_to_all x1, starting transfers between devices, local(): lax.all_to_all(outgoing, 'dp', split_axis=0, concat_axis=0, tiled=True)  6.35 us
    dot_general x1, matrix products, local(): combined = jnp.einsum('rhgk,khd->rhgd', weights, prompt_values) / weight_sum  5.72 us
  transfers between devices with their start and end apart: 4, of which 3 were waited for; matrix products, arithmetic and copies ran while one was open for 16% of the time, Pallas kernels for 0%

commit v1 on v0

v1 whole, which is shorter than its diff:
```python
import functools
import math

import jax
import jax.numpy as jnp
from jax import lax
from jax.experimental import pallas as pl
from jax.experimental.pallas import tpu as pltpu
from jax.sharding import PartitionSpec as P

HD = 128
LANES = 128
F32 = jnp.float32
BF16 = jnp.bfloat16
HIDDEN = -1e30
MIB = 1 << 20
NT = (((1,), (1,)), ((), ()))


def params(mib):
    return pltpu.CompilerParams(vmem_limit_bytes=mib * MIB)


def cost(flops, nbytes, exps=0):
    return pl.CostEstimate(flops=flops, bytes_accessed=nbytes, transcendentals=exps)


def whole(count):
    return [pl.BlockSpec(memory_space=pltpu.VMEM)] * count


def slots(routes_ref, count, owners, capacity, base):
    names = [routes_ref[c] for c in range(count)]
    found = []
    for c in range(count):
        rank = jnp.int32(0)
        for earlier in range(c):
            rank = rank + (names[earlier] == names[c]).astype(jnp.int32)
        owner = names[c] - base
        owner = jnp.where(owner < 0, owner + owners, owner)
        found.append(owner * capacity + rank)
    return found


def spread(scalars, shape, dim):
    index = lax.broadcasted_iota(jnp.int32, shape, dim)
    out = jnp.full(shape, -1, jnp.int32)
    for c, value in enumerate(scalars):
        out = jnp.where(index == c, value, out)
    return out


def pack_kernel(owners, capacity, relative, routes_ref, q_ref, *out_refs):
    steps, count, _ = q_ref.shape
    base = lax.axis_index("dp") if relative else 0
    found = slots(routes_ref, count, owners, capacity, base)
    shape = (owners * capacity, count)
    placement = (spread(found, shape, 1) == lax.broadcasted_iota(jnp.int32, shape, 0)).astype(BF16)
    for s in range(steps):
        rows = jnp.dot(placement, q_ref[s], preferred_element_type=F32)
        at = 0
        for ref in out_refs:
            ref[s] = rows[at : at + ref.shape[1]].astype(BF16)
            at += ref.shape[1]


def suffix_kernel(
    group, len_ref, q_ref, k_ref, v_ref, nk_ref, nv_ref, o_ref, l_ref, qs, ss, ps, os, ls
):
    steps, count, width = q_ref.shape
    heads = width // HD // group
    cached = k_ref.shape[1]
    each = steps * group
    rows = count * each
    scale = 1.0 / math.sqrt(HD)
    to_two = scale * math.log2(math.e)
    for h in range(heads):
        for s in range(steps):
            for g in range(group):
                piece = q_ref[s, :, pl.ds((h * group + g) * HD, HD)].astype(F32)
                qs[pl.ds(h * rows + s * group + g, count, stride=each), :] = piece
    row = lax.broadcasted_iota(jnp.int32, (rows, steps * count), 0).astype(F32)
    column = lax.broadcasted_iota(jnp.int32, (rows, steps * count), 1).astype(F32)
    row_cand = jnp.floor((row + 0.5) * (1.0 / each))
    row_step = jnp.floor((row - row_cand * each + 0.5) * (1.0 / group))
    key_step = jnp.floor((column + 0.5) * (1.0 / count))
    key_cand = column - key_step * count
    visible = (row_cand == key_cand) & (key_step <= row_step)
    position = lax.broadcasted_iota(jnp.int32, (each, cached), 1)
    for h in range(heads):
        for c in range(count):
            qc = qs[pl.ds(h * rows + c * each, each), :].astype(BF16)
            kc = k_ref[c, :, pl.ds(h * HD, HD)]
            score = lax.dot_general(qc, kc, NT, preferred_element_type=F32)
            ss[pl.ds(c * each, each), :] = jnp.where(position < len_ref[c], score, HIDDEN)
        nk = jnp.concatenate([nk_ref[t, :, pl.ds(h * HD, HD)] for t in range(steps)], 0)
        nv = jnp.concatenate([nv_ref[t, :, pl.ds(h * HD, HD)] for t in range(steps)], 0)
        fresh = lax.dot_general(
            qs[pl.ds(h * rows, rows), :].astype(BF16), nk, NT, preferred_element_type=F32
        )
        fresh = jnp.where(visible, fresh, HIDDEN)
        score = ss[...]
        peak = jnp.maximum(
            jnp.max(score, -1, keepdims=True), jnp.max(fresh, -1, keepdims=True)
        )
        weight = jnp.exp2((score - peak) * to_two)
        fresh = jnp.exp2((fresh - peak) * to_two)
        total = jnp.sum(weight, -1, keepdims=True) + jnp.sum(fresh, -1, keepdims=True)
        ps[...] = weight.astype(BF16)
        os[...] = jnp.dot(fresh.astype(BF16), nv, preferred_element_type=F32)
        for c in range(count):
            vc = v_ref[c, :, pl.ds(h * HD, HD)]
            pc = ps[pl.ds(c * each, each), :]
            os[pl.ds(c * each, each), :] += jnp.dot(pc, vc, preferred_element_type=F32)
        os[...] = os[...] / total
        ls[...] = jnp.broadcast_to(peak * scale + jnp.log(total), ls.shape)
        for s in range(steps):
            for g in range(group):
                at = pl.ds(s * group + g, count, stride=each)
                lanes = pl.ds((h * group + g) * HD, HD)
                o_ref[s, :, lanes] = os[at, :]
                l_ref[s, :, lanes] = ls[at, :]


def prompt_kernel(group, blocks, *refs):
    q_refs, (k_ref, v_ref), out_refs = refs[:blocks], refs[blocks : blocks + 2], refs[blocks + 2 :]
    steps, _, width = q_refs[0].shape
    heads = width // HD // group
    all_heads = heads * group
    scale = 1.0 / math.sqrt(HD)
    to_two = scale * math.log2(math.e)
    for q_ref, out_ref in zip(q_refs, out_refs, strict=True):
        size = q_ref.shape[1]
        lane = lax.broadcasted_iota(jnp.int32, (size, LANES), 1)
        place = lax.rem(lane, all_heads)
        logs = [jnp.zeros((size, LANES), F32) for _ in range(steps)]
        for h in range(heads):
            keys = k_ref[:, pl.ds(h * HD, HD)]
            values = v_ref[:, pl.ds(h * HD, HD)]
            q = jnp.concatenate(
                [
                    q_ref[s, :, pl.ds((h * group + g) * HD, HD)]
                    for s in range(steps)
                    for g in range(group)
                ],
                0,
            )
            score = lax.dot_general(q, keys, NT, preferred_element_type=F32)
            peak = jnp.max(score, -1, keepdims=True)
            weight = jnp.exp2((score - peak) * to_two)
            total = jnp.sum(weight, -1, keepdims=True)
            out = jnp.dot(weight.astype(BF16), values, preferred_element_type=F32) / total
            log_total = peak * scale + jnp.log(total)
            for s in range(steps):
                for g in range(group):
                    at = (s * group + g) * size
                    out_ref[s, :, pl.ds((h * group + g) * HD, HD)] = out[at : at + size].astype(
                        BF16
                    )
                    logs[s] = jnp.where(
                        place == h * group + g, log_total[at : at + size], logs[s]
                    )
        for s in range(steps):
            high = logs[s].astype(BF16).astype(F32)
            rest = logs[s] - high
            middle = rest.astype(BF16).astype(F32)
            low = rest - middle
            terms = jnp.where(
                lane < all_heads, high, jnp.where(lane < 2 * all_heads, middle, low)
            )
            out_ref[s, :, pl.ds(width, LANES)] = terms.astype(BF16)


def merge_kernel(owners, capacity, relative, blocks, *refs):
    routes_ref, row_refs = refs[0], refs[1 : 1 + blocks]
    own_ref, log_ref, out_ref = refs[1 + blocks :]
    steps, count, width = own_ref.shape
    all_heads = width // HD
    base = lax.axis_index("dp") if relative else 0
    found = slots(routes_ref, count, owners, capacity, base)
    shape = (count, owners * capacity)
    choice = (spread(found, shape, 0) == lax.broadcasted_iota(jnp.int32, shape, 1)).astype(BF16)
    for s in range(steps):
        rows = jnp.concatenate([ref[s] for ref in row_refs], 0)
        rows = jnp.dot(choice, rows, preferred_element_type=F32)
        terms = rows[:, width:]
        logs = (
            terms[:, :all_heads]
            + terms[:, all_heads : 2 * all_heads]
            + terms[:, 2 * all_heads : 3 * all_heads]
        )
        for h in range(all_heads):
            lanes = slice(h * HD, (h + 1) * HD)
            first = jnp.broadcast_to(logs[:, h : h + 1], (count, HD))
            second = log_ref[s, :, lanes]
            peak = jnp.maximum(first, second)
            first = jnp.exp(first - peak)
            second = jnp.exp(second - peak)
            mixed = (first * rows[:, lanes] + second * own_ref[s, :, lanes]) / (first + second)
            out_ref[s, :, lanes] = mixed.astype(BF16)


def project_kernel(owners, parts, *refs):
    rows_refs, w_ref, own_ref, send_refs, held = (
        refs[:owners],
        refs[owners],
        refs[owners + 1],
        refs[owners + 2 : -1],
        refs[-1],
    )
    steps, count, _ = rows_refs[0].shape
    each = steps * count

    @pl.when(pl.program_id(0) == 0)
    def _():
        me, mine = lax.axis_index("dp"), lax.axis_index("kv")
        for shift, ref in enumerate(rows_refs):
            place = lax.rem(me - shift - mine + owners + parts, parts)
            for s in range(steps):
                held[place, pl.ds(s * count, count), :] = ref[s]

    product = jnp.dot(
        held[...].reshape(parts * each, held.shape[2]), w_ref[...], preferred_element_type=F32
    )
    for part, ref in enumerate((own_ref, *send_refs)):
        for s in range(steps):
            at = part * each + s * count
            ref[s] = product[at : at + count].astype(ref.dtype)


def shift_by(values, axis, amount):
    size = lax.axis_size(axis)
    return lax.ppermute(values, axis, [(i, (i + amount) % size) for i in range(size)])


def local(
    queries,
    routes,
    suffix_lengths,
    prefix_keys,
    prefix_values,
    suffix_keys,
    suffix_values,
    new_keys,
    new_values,
    out_weight,
):
    owners, parts = lax.axis_size("dp"), lax.axis_size("kv")
    count, steps, width = queries.shape
    kv_width = prefix_keys.shape[2]
    heads = kv_width // HD
    group = width // kv_width
    capacity = max(2, 2 * count // owners)
    direct = owners == parts and capacity % 8 == 0
    blocks = owners if direct else 1
    size = capacity if direct else owners * capacity
    smem = pl.BlockSpec(memory_space=pltpu.SMEM)
    q = queries.transpose(1, 0, 2)
    names = routes.reshape(count)

    packed = pl.pallas_call(
        functools.partial(pack_kernel, owners, capacity, direct),
        out_shape=[jax.ShapeDtypeStruct((steps, size, width), BF16)] * blocks,
        in_specs=[smem, *whole(1)],
        out_specs=whole(blocks),
        compiler_params=params(16),
        cost_estimate=cost(2 * steps * owners * capacity * count * width, 1 << 20),
        name="pack",
    )(names, q)

    def exchange(arrays, back):
        if direct:
            sign = -1 if back else 1
            return [arrays[0]] + [
                shift_by(values, "dp", sign * shift)
                for shift, values in enumerate(arrays)
                if shift
            ]
        values = arrays[0].reshape(steps, owners, capacity, -1)
        moved = lax.all_to_all(values, "dp", split_axis=1, concat_axis=1, tiled=True)
        return [moved.reshape(steps, owners * capacity, -1)]

    received = exchange(packed, False)

    rows = count * steps * group
    own_rows, own_logs = pl.pallas_call(
        functools.partial(suffix_kernel, group),
        out_shape=[jax.ShapeDtypeStruct((steps, count, width), F32)] * 2,
        in_specs=[smem, *whole(5)],
        out_specs=whole(2),
        scratch_shapes=[
            pltpu.VMEM((heads * rows, HD), F32),
            pltpu.VMEM((rows, suffix_keys.shape[1]), F32),
            pltpu.VMEM((rows, suffix_keys.shape[1]), BF16),
            pltpu.VMEM((rows, HD), F32),
            pltpu.VMEM((rows, LANES), F32),
        ],
        compiler_params=params(24),
        cost_estimate=cost(
            4 * heads * rows * suffix_keys.shape[1] * HD * 8, suffix_keys.size * 4, rows * 512
        ),
        name="suffix",
    )(
        suffix_lengths,
        q,
        suffix_keys,
        suffix_values,
        new_keys.transpose(1, 0, 2),
        new_values.transpose(1, 0, 2),
    )

    returned = pl.pallas_call(
        functools.partial(prompt_kernel, group, blocks),
        out_shape=[jax.ShapeDtypeStruct((steps, size, width + LANES), BF16)] * blocks,
        in_specs=whole(blocks + 2),
        out_specs=whole(blocks),
        compiler_params=params(40),
        cost_estimate=cost(
            4 * owners * capacity * steps * width * prefix_keys.shape[1], prefix_keys.size * 4
        ),
        name="prompt",
    )(*received, prefix_keys[0], prefix_values[0])
    home = exchange(returned, True)

    attended = pl.pallas_call(
        functools.partial(merge_kernel, owners, capacity, direct, blocks),
        out_shape=jax.ShapeDtypeStruct((steps, count, width), BF16),
        in_specs=[smem, *whole(blocks + 2)],
        out_specs=whole(1)[0],
        compiler_params=params(16),
        cost_estimate=cost(2 * steps * owners * capacity * count * width, 2 << 20),
        name="merge",
    )(names, *home, own_rows, own_logs)

    columns = out_weight.shape[1]
    if not direct:
        block_rows = lax.all_gather(attended, "dp", axis=1, tiled=True)
        product = jnp.dot(
            block_rows.reshape(-1, width), out_weight, preferred_element_type=F32
        ).reshape(steps, -1, columns)
        total = lax.psum_scatter(product, "kv", scatter_dimension=1, tiled=True)
        return total.astype(BF16).transpose(1, 0, 2)

    gathered = [attended] + [shift_by(attended, "dp", shift) for shift in range(1, owners)]
    chunk = columns // 4
    own_sum, *sent = pl.pallas_call(
        functools.partial(project_kernel, owners, parts),
        grid=(columns // chunk,),
        out_shape=[jax.ShapeDtypeStruct((steps, count, columns), F32)]
        + [jax.ShapeDtypeStruct((steps, count, columns), BF16)] * (parts - 1),
        in_specs=[pl.BlockSpec((steps, count, width), lambda i: (0, 0, 0))] * owners
        + [pl.BlockSpec((width, chunk), lambda i: (0, i))],
        out_specs=[pl.BlockSpec((steps, count, chunk), lambda i: (0, 0, i))] * parts,
        scratch_shapes=[pltpu.VMEM((parts, steps * count, width), BF16)],
        compiler_params=params(24),
        cost_estimate=cost(2 * owners * steps * count * width * columns, out_weight.size * 2),
        name="project",
    )(*gathered, out_weight)
    total = own_sum
    for shift, values in enumerate(sent, 1):
        total = total + shift_by(values, "kv", shift).astype(F32)
    return total.astype(BF16).transpose(1, 0, 2)


def solution(mesh):
    placed = (
        P(("groups", "dp"), None, "kv"),
        P(("groups", "dp"), None),
        P(("groups", "dp")),
        P(("groups", "dp"), None, "kv"),
        P(("groups", "dp"), None, "kv"),
        P(("groups", "dp"), None, "kv"),
        P(("groups", "dp"), None, "kv"),
        P(("groups", "dp"), None, "kv"),
        P(("groups", "dp"), None, "kv"),
        P("kv", "dp"),
    )
    return jax.shard_map(
        local,
        mesh=mesh,
        in_specs=placed,
        out_specs=P(("groups", "kv"), None, "dp"),
        check_vma=False,
    )
```

time: 143 us -> 70.9 us (0.50)
  matrix products: 24.2 us -> 0 us
  blocking collectives: 17.7 us -> 0 us
  between operations: 13.7 us -> 0.07 us
  Pallas kernels: 0 us -> 12.9 us
  other arithmetic: 13.2 us -> 0.76 us
  waiting for transfers between devices: 42.5 us -> 30.6 us
  local copies, waits for them, and re-layouts: 16.8 us -> 8.69 us
  starting transfers between devices: 14.6 us -> 17.2 us
    ppermute x0 -> x12, waiting for transfers between devices: none -> 30.6 us  [shift_by(): lax.ppermute(values, axis, [(i, (i + amount) % size) for i in range(size)])]
    reduce_scatter x1 -> x0, waiting for transfers between devices: 27.8 us -> none  [local(): lax.psum_scatter(partial_value, 'kv', scatter_dimension=0, tiled=True)]
    dot_general x7 -> x0, matrix products: 24.2 us -> none  [the longest x1 6.38 us: local(): jnp.einsum('rhgd,khd->rhgk', query_heads, prompt_keys, preferred_element_...]
    all_gather x1 -> x0, blocking collectives: 17.7 us -> none  [local(): block_rows = lax.all_gather(attended, 'dp', axis=0, tiled=True)]
    ppermute x0 -> x12, starting transfers between devices: none -> 17.2 us  [shift_by(): lax.ppermute(values, axis, [(i, (i + amount) % size) for i in range(size)])]
    all_to_all x3 -> x0, waiting for transfers between devices: 14.7 us -> none  [the longest x1 9.21 us: local(): lax.all_to_all(outgoing, 'dp', split_axis=0, concat_axis=0, tiled=True)]
    all_to_all x3 -> x0, starting transfers between devices: 14.6 us -> none  [the longest x1 6.35 us: local(): lax.all_to_all(outgoing, 'dp', split_axis=0, concat_axis=0, tiled=True)]
    pallas_call x0 -> x5, Pallas kernels: none -> 12.9 us  [the longest x1 5.25 us: local(): pl.pallas_call(functools.partial(prompt_kernel, group, blocks), out_shape...]
  transfers between devices with their start and end apart: 4 -> 12, of which waited for: 3 -> 8; matrix products, arithmetic and copies ran while one was open for 16% -> 0% of each run, Pallas kernels for 0% -> 3%
where the time goes in v1:
time: 70.9 us; the launch traced here: 70.1 us
  waiting for transfers between devices  30.6 us (43%)
  starting transfers between devices  17.2 us (24%)
  Pallas kernels  12.9 us (18%)
  local copies, waits for them, and re-layouts  8.69 us (12%)
  other arithmetic  0.76 us (1%)
    ppermute x12, waiting for transfers between devices, shift_by(): lax.ppermute(values, axis, [(i, (i + amount) % size) for i in range(size)])  30.6 us
    ppermute x12, starting transfers between devices, shift_by(): lax.ppermute(values, axis, [(i, (i + amount) % size) for i in range(size)])  17.2 us
    unnamed x24, local copies, waits for them, and re-layouts  8.69 us
    pallas_call x1, Pallas kernels, local(): pl.pallas_call(functools.partial(prompt_kernel, group, blocks), out_shape...  5.25 us
    pallas_call x1, Pallas kernels, local(): pl.pallas_call(functools.partial(project_kernel, owners, parts), grid=(co...  3.22 us
    pallas_call x1, Pallas kernels, local(): pl.pallas_call(functools.partial(suffix_kernel, group), out_shape=[jax.Sh...  2.28 us
  transfers between devices with their start and end apart: 12, of which 8 were waited for; matrix products, arithmetic and copies ran while one was open for 0% of the time, Pallas kernels for 3%

profile of v1, /device:TPU:0, one launch (start us, length us, event | category | flops | bytes accessed | tf_op | source)
XLA Modules:
  0.0 70.1 jit_solution(15410397080080201510)
XLA Ops:
  0.0 0.0 copy-start.3
  0.0 0.9 %copy-done.3 = bf16[16,3,2048]{2,0,1:T(8,128)(2,1)S(1)} copy-done((bf16[16,3,2048]{2,0,1:T(8,128)(2,1)S(1)}, bf16[16,3,2048]{2,0,1:T(8,128)(2,1)}, u32[]{:S(2)}) %copy-start.3) | copy-done | bytes 196632
  0.9 0.0 copy-start.7
  0.9 0.7 copy-done.7
  1.6 0.0 copy-start.1
  1.6 0.9 %pack.1 = (bf16[3,8,2048]{2,1,0:T(8,128)(2,1)S(1)}, bf16[3,8,2048]{2,1,0:T(8,128)(2,1)S(1)}, bf16[3,8,2048]{2,1,0:T(8,128)(2,1)S(1)}, bf16[3,8,2048]{2,1,0:T(8,128)(2,1)S(1)}) custom-call(s32[16]{0:T(128)S(1)} %bitcast.12, bf16[3,16,2048]{2,1,0:T(8,128)(2,1)S(1)} %bitcast.8), custom_call_target="tpu_custom_call" | custom-call | flops 6291456 | bytes 1048576 | tf_op jit(solution)/shard_map/pack/pallas_call | solution.py:261
  2.5 3.1 %collective-permute-start = (bf16[3,8,2048]{2,1,0:T(8,128)(2,1)S(1)}, bf16[3,8,2048]{2,1,0:T(8,128)(2,1)S(1)}, u32[]{:S(2)}, u32[]{:S(2)}) collective-permute-start(bf16[3,8,2048]{2,1,0:T(8,128)(2,1)S(1)} %get-tuple-element.20), channel_id=1, source_target_pairs={{0,4},{4,8},{8,12},{12,0},{1,5},{5,9},{9,13},{13,1},{2,6},{6,10},{... | collective-permute-start | bytes 294920 | tf_op jit(solution)/shard_map/ppermute | solution.py:233
  5.6 2.6 %collective-permute-start.1 = (bf16[3,8,2048]{2,1,0:T(8,128)(2,1)S(1)}, bf16[3,8,2048]{2,1,0:T(8,128)(2,1)S(1)}, u32[]{:S(2)}, u32[]{:S(2)}) collective-permute-start(bf16[3,8,2048]{2,1,0:T(8,128)(2,1)S(1)} %get-tuple-element.21), channel_id=1, source_target_pairs={{0,8},{4,12},{8,0},{12,4},{1,9},{5,13},{9,1},{13,5},{2,10},{6,14},... | collective-permute-start | bytes 294920 | tf_op jit(solution)/shard_map/ppermute | solution.py:233
  8.2 1.4 %collective-permute-start.2 = (bf16[3,8,2048]{2,1,0:T(8,128)(2,1)S(1)}, bf16[3,8,2048]{2,1,0:T(8,128)(2,1)S(1)}, u32[]{:S(2)}, u32[]{:S(2)}) collective-permute-start(bf16[3,8,2048]{2,1,0:T(8,128)(2,1)S(1)} %get-tuple-element.22), channel_id=1, source_target_pairs={{0,12},{4,0},{8,4},{12,8},{1,13},{5,1},{9,5},{13,9},{2,14},{6,2},{... | collective-permute-start | bytes 294920 | tf_op jit(solution)/shard_map/ppermute | solution.py:233
  9.6 1.7 %collective-permute-done.refs_1_ = bf16[3,8,2048]{2,1,0:T(8,128)(2,1)S(1)} collective-permute-done((bf16[3,8,2048]{2,1,0:T(8,128)(2,1)S(1)}, bf16[3,8,2048]{2,1,0:T(8,128)(2,1)S(1)}, u32[]{:S(2)}, u32[]{:S(2)}) %collective-permute-start) | collective-permute-done | bytes 98336 | tf_op jit(solution)/shard_map/ppermute | solution.py:233
  11.3 3.5 %collective-permute-done.1.refs_2_ = bf16[3,8,2048]{2,1,0:T(8,128)(2,1)S(1)} collective-permute-done((bf16[3,8,2048]{2,1,0:T(8,128)(2,1)S(1)}, bf16[3,8,2048]{2,1,0:T(8,128)(2,1)S(1)}, u32[]{:S(2)}, u32[]{:S(2)}) %collective-permute-start.1) | collective-permute-done | bytes 98336 | tf_op jit(solution)/shard_map/ppermute | solution.py:233
  14.8 0.0 collective-permute-done.2.refs_3_
  14.8 0.0 copy-start.10
  14.8 1.2 %copy-done.10 = bf16[1,2048,256]{2,1,0:T(8,128)(2,1)S(1)} copy-done((bf16[1,2048,256]{2,1,0:T(8,128)(2,1)S(1)}, bf16[1,2048,256]{2,1,0:T(8,128)(2,1)}, u32[]{:S(2)}) %copy-start.10) | copy-done | bytes 1048600
  16.1 0.0 copy-start.11
  16.1 1.2 %copy-done.11 = bf16[1,2048,256]{2,1,0:T(8,128)(2,1)S(1)} copy-done((bf16[1,2048,256]{2,1,0:T(8,128)(2,1)S(1)}, bf16[1,2048,256]{2,1,0:T(8,128)(2,1)}, u32[]{:S(2)}) %copy-start.11) | copy-done | bytes 1048600
  17.3 0.0 copy-start
  17.3 5.2 %prompt.1 = (bf16[3,8,2176]{2,1,0:T(8,128)(2,1)S(1)}, bf16[3,8,2176]{2,1,0:T(8,128)(2,1)S(1)}, bf16[3,8,2176]{2,1,0:T(8,128)(2,1)S(1)}, bf16[3,8,2176]{2,1,0:T(8,128)(2,1)S(1)}) custom-call(bf16[3,8,2048]{2,1,0:T(8,128)(2,1)S(1)} %get-tuple-element.19.refs_0_, bf16[3,8,2048]{2,1,0:T(8,128)(2,1)S(1)} %collective-permute-done.refs_1_, ...), custom_call_target="tpu_custom_call" | custom-call | flops 1610612736 | bytes 2097152 | tf_op jit(solution)/shard_map/prompt/pallas_call | solution.py:312
  22.5 3.6 %collective-permute-start.3 = (bf16[3,8,2176]{2,1,0:T(8,128)(2,1)S(1)}, bf16[3,8,2176]{2,1,0:T(8,128)(2,1)S(1)}, u32[]{:S(2)}, u32[]{:S(2)}) collective-permute-start(bf16[3,8,2176]{2,1,0:T(8,128)(2,1)S(1)} %get-tuple-element.24), channel_id=1, source_target_pairs={{0,12},{4,0},{8,4},{12,8},{1,13},{5,1},{9,5},{13,9},{2,14},{6,2},{... | collective-permute-start | bytes 313352 | tf_op jit(solution)/shard_map/ppermute | solution.py:233
  26.2 0.4 collective-permute-start.4
  26.6 0.2 collective-permute-start.5
  26.8 0.0 copy-done.1
  26.8 1.6 %copy-done.2 = bf16[16,256,256]{2,1,0:T(8,128)(2,1)S(1)} copy-done((bf16[16,256,256]{2,1,0:T(8,128)(2,1)S(1)}, bf16[16,256,256]{2,1,0:T(8,128)(2,1)}, u32[]{:S(2)}) %copy-start.2) | copy-done | bytes 2097176
  28.4 0.9 %copy-done.4 = bf16[16,3,2048]{2,0,1:T(8,128)(2,1)S(1)} copy-done((bf16[16,3,2048]{2,0,1:T(8,128)(2,1)S(1)}, bf16[16,3,2048]{2,0,1:T(8,128)(2,1)}, u32[]{:S(2)}) %copy-start.4) | copy-done | bytes 196632
  29.4 0.7 %copy-done.5 = bf16[16,3,256]{2,0,1:T(8,128)(2,1)S(1)} copy-done((bf16[16,3,256]{2,0,1:T(8,128)(2,1)S(1)}, bf16[16,3,256]{2,0,1:T(8,128)(2,1)}, u32[]{:S(2)}) %copy-start.5) | copy-done | bytes 24600
  30.1 0.7 %copy-done.6 = bf16[16,3,256]{2,0,1:T(8,128)(2,1)S(1)} copy-done((bf16[16,3,256]{2,0,1:T(8,128)(2,1)S(1)}, bf16[16,3,256]{2,0,1:T(8,128)(2,1)}, u32[]{:S(2)}) %copy-start.6) | copy-done | bytes 24600
  30.8 0.7 copy-done.9
  31.5 2.3 %suffix.1 = (f32[3,16,2048]{2,1,0:T(8,128)S(1)}, f32[3,16,2048]{2,1,0:T(8,128)S(1)}) custom-call(s32[16]{0:T(128)S(1)} %copy-done.9, bf16[3,16,2048]{2,1,0:T(8,128)(2,1)S(1)} %bitcast.9, bf16[16,256,256]{2,1,0:T(8,128)(2,1)S(1)} %copy-done.1, bf16[16,256,256]{2,1,0:T(8,128)(2,1)S(1)} %copy-done.2, bf16[3,16,256]{2,1,0:T(8,128)(2,1)S(1)} %bitcast.10, ...), custom_call_target="tpu_custom_call" | custom-call | flops 805306368 | bytes 4194304 | tf_op jit(solution)/shard_map/suffix/pallas_call | solution.py:286
  33.8 0.0 collective-permute-done.3.refs_2_
  33.8 2.3 %collective-permute-done.4.refs_3_ = bf16[3,8,2176]{2,1,0:T(8,128)(2,1)S(1)} collective-permute-done((bf16[3,8,2176]{2,1,0:T(8,128)(2,1)S(1)}, bf16[3,8,2176]{2,1,0:T(8,128)(2,1)S(1)}, u32[]{:S(2)}, u32[]{:S(2)}) %collective-permute-start.4) | collective-permute-done | bytes 104480 | tf_op jit(solution)/shard_map/ppermute | solution.py:233
  36.1 0.0 collective-permute-done.5.refs_4_
  36.1 0.0 copy-done.8
  36.1 1.2 %merge.1.refs_0_ = bf16[3,16,2048]{2,1,0:T(8,128)(2,1)S(1)} custom-call(s32[16]{0:T(128)S(1)} %bitcast.13, bf16[3,8,2176]{2,1,0:T(8,128)(2,1)S(1)} %get-tuple-element.23.refs_1_, bf16[3,8,2176]{2,1,0:T(8,128)(2,1)S(1)} %collective-permute-done.3.refs_2_, bf16[3,8,2176]{2,1,0:T(8,128)(2,1)S(1)} %collective-permute-done.4.refs_3_, ...), custom_call_target="tpu_custom_call" | custom-call | flops 6291456 | bytes 2097152 | tf_op jit(solution)/shard_map/merge/pallas_call | solution.py:325
  37.3 1.3 %collective-permute-start.8 = (bf16[3,16,2048]{2,1,0:T(8,128)(2,1)S(1)}, bf16[3,16,2048]{2,1,0:T(8,128)(2,1)S(1)}, u32[]{:S(2)}, u32[]{:S(2)}) collective-permute-start(bf16[3,16,2048]{2,1,0:T(8,128)(2,1)S(1)} %merge.1.refs_0_), channel_id=1, source_target_pairs={{0,12},{4,0},{8,4},{12,8},{1,13},{5,1},{9,5},{13,9},{2,14},{6,2},{... | collective-permute-start | bytes 589832 | tf_op jit(solution)/shard_map/ppermute | solution.py:233
  38.7 0.7 %collective-permute-start.7 = (bf16[3,16,2048]{2,1,0:T(8,128)(2,1)S(1)}, bf16[3,16,2048]{2,1,0:T(8,128)(2,1)S(1)}, u32[]{:S(2)}, u32[]{:S(2)}) collective-permute-start(bf16[3,16,2048]{2,1,0:T(8,128)(2,1)S(1)} %merge.1.refs_0_), channel_id=1, source_target_pairs={{0,8},{4,12},{8,0},{12,4},{1,9},{5,13},{9,1},{13,5},{2,10},{6,14},... | collective-permute-start | bytes 589832 | tf_op jit(solution)/shard_map/ppermute | solution.py:233
  39.4 0.8 %collective-permute-start.6 = (bf16[3,16,2048]{2,1,0:T(8,128)(2,1)S(1)}, bf16[3,16,2048]{2,1,0:T(8,128)(2,1)S(1)}, u32[]{:S(2)}, u32[]{:S(2)}) collective-permute-start(bf16[3,16,2048]{2,1,0:T(8,128)(2,1)S(1)} %merge.1.refs_0_), channel_id=1, source_target_pairs={{0,4},{4,8},{8,12},{12,0},{1,5},{5,9},{9,13},{13,1},{2,6},{6,10},{... | collective-permute-start | bytes 589832 | tf_op jit(solution)/shard_map/ppermute | solution.py:233
  40.2 4.3 %collective-permute-done.8.refs_3_ = bf16[3,16,2048]{2,1,0:T(8,128)(2,1)S(1)} collective-permute-done((bf16[3,16,2048]{2,1,0:T(8,128)(2,1)S(1)}, bf16[3,16,2048]{2,1,0:T(8,128)(2,1)S(1)}, u32[]{:S(2)}, u32[]{:S(2)}) %collective-permute-start.8) | collective-permute-done | bytes 196640 | tf_op jit(solution)/shard_map/ppermute | solution.py:233
  44.5 11.2 %collective-permute-done.7.refs_2_ = bf16[3,16,2048]{2,1,0:T(8,128)(2,1)S(1)} collective-permute-done((bf16[3,16,2048]{2,1,0:T(8,128)(2,1)S(1)}, bf16[3,16,2048]{2,1,0:T(8,128)(2,1)S(1)}, u32[]{:S(2)}, u32[]{:S(2)}) %collective-permute-start.7) | collective-permute-done | bytes 196640 | tf_op jit(solution)/shard_map/ppermute | solution.py:233
  55.7 0.0 collective-permute-done.6.refs_1_
  55.7 0.0 copy-done
  55.7 3.2 %project.1 = (f32[3,16,2048]{2,1,0:T(8,128)S(1)}, bf16[3,16,2048]{2,1,0:T(8,128)(2,1)S(1)}, bf16[3,16,2048]{2,1,0:T(8,128)(2,1)S(1)}, bf16[3,16,2048]{2,1,0:T(8,128)(2,1)S(1)}) custom-call(bf16[3,16,2048]{2,1,0:T(8,128)(2,1)S(1)} %merge.1.refs_0_, bf16[3,16,2048]{2,1,0:T(8,128)(2,1)S(1)} %collective-permute-done.6.refs_1_, ...), custom_call_target="tpu_custom_call" | custom-call | flops 1610612736 | bytes 8388608 | tf_op jit(solution)/shard_map/project/pallas_call | solution.py:346
  58.9 0.1 collective-permute-start.9
  59.0 1.6 %collective-permute-start.10 = (bf16[3,16,2048]{2,1,0:T(8,128)(2,1)S(1)}, bf16[3,16,2048]{2,1,0:T(8,128)(2,1)S(1)}, u32[]{:S(2)}, u32[]{:S(2)}) collective-permute-start(bf16[3,16,2048]{2,1,0:T(8,128)(2,1)S(1)} %get-tuple-element.31), channel_id=1, source_target_pairs={{0,2},{1,3},{2,0},{3,1},{4,6},{5,7},{6,4},{7,5},{8,10},{9,11},{10,... | collective-permute-start | bytes 589832 | tf_op jit(solution)/shard_map/ppermute | solution.py:233
  60.5 1.4 %collective-permute-start.11 = (bf16[3,16,2048]{2,1,0:T(8,128)(2,1)S(1)}, bf16[3,16,2048]{2,1,0:T(8,128)(2,1)S(1)}, u32[]{:S(2)}, u32[]{:S(2)}) collective-permute-start(bf16[3,16,2048]{2,1,0:T(8,128)(2,1)S(1)} %get-tuple-element.32), channel_id=1, source_target_pairs={{0,3},{1,0},{2,1},{3,2},{4,7},{5,4},{6,5},{7,6},{8,11},{9,8},{10,9... | collective-permute-start | bytes 589832 | tf_op jit(solution)/shard_map/ppermute | solution.py:233
  61.9 3.6 %collective-permute-done.9 = bf16[3,16,2048]{2,1,0:T(8,128)(2,1)S(1)} collective-permute-done((bf16[3,16,2048]{2,1,0:T(8,128)(2,1)S(1)}, bf16[3,16,2048]{2,1,0:T(8,128)(2,1)S(1)}, u32[]{:S(2)}, u32[]{:S(2)}) %collective-permute-start.9) | collective-permute-done | bytes 196640 | tf_op jit(solution)/shard_map/ppermute | solution.py:233
  65.5 1.3 %collective-permute-done.10 = bf16[3,16,2048]{2,1,0:T(8,128)(2,1)S(1)} collective-permute-done((bf16[3,16,2048]{2,1,0:T(8,128)(2,1)S(1)}, bf16[3,16,2048]{2,1,0:T(8,128)(2,1)S(1)}, u32[]{:S(2)}, u32[]{:S(2)}) %collective-permute-start.10) | collective-permute-done | bytes 196640 | tf_op jit(solution)/shard_map/ppermute | solution.py:233
  66.8 2.6 %collective-permute-done.11 = bf16[3,16,2048]{2,1,0:T(8,128)(2,1)S(1)} collective-permute-done((bf16[3,16,2048]{2,1,0:T(8,128)(2,1)S(1)}, bf16[3,16,2048]{2,1,0:T(8,128)(2,1)S(1)}, u32[]{:S(2)}, u32[]{:S(2)}) %collective-permute-start.11) | collective-permute-done | bytes 196640 | tf_op jit(solution)/shard_map/ppermute | solution.py:233
  69.4 0.8 %fusion = bf16[16,3,2048]{2,0,1:T(8,128)(2,1)} fusion(bf16[3,16,2048]{2,1,0:T(8,128)(2,1)S(1)} %collective-permute-done.11, bf16[3,16,2048]{2,1,0:T(8,128)(2,1)S(1)} %collective-permute-done.10, f32[3,16,2048]{2,1,0:T(8,128)S(1)} %get-tuple-element.29, bf16[3,16,2048]{2,1,0:T(8,128)(2,1)S(1)} %collective-permute-done.9), kind=kLoop, calls=%fused_computation.1 | loop fusion | flops 688128 | bytes 1179648 | tf_op jit(solution)/shard_map/transpose | solution.py:362
  (6 shorter events, 0.0 us)
Async XLA Ops:
  0.0 0.9 %copy-start.3 = (bf16[16,3,2048]{2,0,1:T(8,128)(2,1)S(1)}, bf16[16,3,2048]{2,0,1:T(8,128)(2,1)}, u32[]{:S(2)}) copy-start(bf16[16,3,2048]{2,0,1:T(8,128)(2,1)} %param.10) | copy-start | bytes 589828
  0.9 0.7 copy-start.7
  1.6 25.2 %copy-start.1 = (bf16[16,256,256]{2,1,0:T(8,128)(2,1)S(1)}, bf16[16,256,256]{2,1,0:T(8,128)(2,1)}, u32[]{:S(2)}) copy-start(bf16[16,256,256]{2,1,0:T(8,128)(2,1)} %k_ref.1) | copy-start | bytes 6291460
  2.5 8.8 %collective-permute-start = (bf16[3,8,2048]{2,1,0:T(8,128)(2,1)S(1)}, bf16[3,8,2048]{2,1,0:T(8,128)(2,1)S(1)}, u32[]{:S(2)}, u32[]{:S(2)}) collective-permute-start(bf16[3,8,2048]{2,1,0:T(8,128)(2,1)S(1)} %get-tuple-element.20), channel_id=1, source_target_pairs={{0,4},{4,8},{8,12},{12,0},{1,5},{5,9},{9,13},{13,1},{2,6},{6,10},{... | collective-permute-start | bytes 294920 | tf_op jit(solution)/shard_map/ppermute | solution.py:233
  5.6 9.2 %collective-permute-start.1 = (bf16[3,8,2048]{2,1,0:T(8,128)(2,1)S(1)}, bf16[3,8,2048]{2,1,0:T(8,128)(2,1)S(1)}, u32[]{:S(2)}, u32[]{:S(2)}) collective-permute-start(bf16[3,8,2048]{2,1,0:T(8,128)(2,1)S(1)} %get-tuple-element.21), channel_id=1, source_target_pairs={{0,8},{4,12},{8,0},{12,4},{1,9},{5,13},{9,1},{13,5},{2,10},{6,14},... | collective-permute-start | bytes 294920 | tf_op jit(solution)/shard_map/ppermute | solution.py:233
  8.2 6.6 %collective-permute-start.2 = (bf16[3,8,2048]{2,1,0:T(8,128)(2,1)S(1)}, bf16[3,8,2048]{2,1,0:T(8,128)(2,1)S(1)}, u32[]{:S(2)}, u32[]{:S(2)}) collective-permute-start(bf16[3,8,2048]{2,1,0:T(8,128)(2,1)S(1)} %get-tuple-element.22), channel_id=1, source_target_pairs={{0,12},{4,0},{8,4},{12,8},{1,13},{5,1},{9,5},{13,9},{2,14},{6,2},{... | collective-permute-start | bytes 294920 | tf_op jit(solution)/shard_map/ppermute | solution.py:233
  14.8 1.2 %copy-start.10 = (bf16[1,2048,256]{2,1,0:T(8,128)(2,1)S(1)}, bf16[1,2048,256]{2,1,0:T(8,128)(2,1)}, u32[]{:S(2)}) copy-start(bf16[1,2048,256]{2,1,0:T(8,128)(2,1)} %param.13) | copy-start | bytes 3145732
  16.1 1.2 %copy-start.11 = (bf16[1,2048,256]{2,1,0:T(8,128)(2,1)S(1)}, bf16[1,2048,256]{2,1,0:T(8,128)(2,1)}, u32[]{:S(2)}) copy-start(bf16[1,2048,256]{2,1,0:T(8,128)(2,1)} %param.14) | copy-start | bytes 3145732
  17.3 38.4 %copy-start = (bf16[2048,2048]{1,0:T(8,128)(2,1)S(1)}, bf16[2048,2048]{1,0:T(8,128)(2,1)}, u32[]{:S(2)}) copy-start(bf16[2048,2048]{1,0:T(8,128)(2,1)} %refs_4_.1) | copy-start | bytes 25165828
  22.5 11.2 %collective-permute-start.3 = (bf16[3,8,2176]{2,1,0:T(8,128)(2,1)S(1)}, bf16[3,8,2176]{2,1,0:T(8,128)(2,1)S(1)}, u32[]{:S(2)}, u32[]{:S(2)}) collective-permute-start(bf16[3,8,2176]{2,1,0:T(8,128)(2,1)S(1)} %get-tuple-element.24), channel_id=1, source_target_pairs={{0,12},{4,0},{8,4},{12,8},{1,13},{5,1},{9,5},{13,9},{2,14},{6,2},{... | collective-permute-start | bytes 313352 | tf_op jit(solution)/shard_map/ppermute | solution.py:233
  26.2 9.9 %collective-permute-start.4 = (bf16[3,8,2176]{2,1,0:T(8,128)(2,1)S(1)}, bf16[3,8,2176]{2,1,0:T(8,128)(2,1)S(1)}, u32[]{:S(2)}, u32[]{:S(2)}) collective-permute-start(bf16[3,8,2176]{2,1,0:T(8,128)(2,1)S(1)} %get-tuple-element.25), channel_id=1, source_target_pairs={{0,8},{4,12},{8,0},{12,4},{1,9},{5,13},{9,1},{13,5},{2,10},{6,14},... | collective-permute-start | bytes 313352 | tf_op jit(solution)/shard_map/ppermute | solution.py:233
  26.6 9.5 %collective-permute-start.5 = (bf16[3,8,2176]{2,1,0:T(8,128)(2,1)S(1)}, bf16[3,8,2176]{2,1,0:T(8,128)(2,1)S(1)}, u32[]{:S(2)}, u32[]{:S(2)}) collective-permute-start(bf16[3,8,2176]{2,1,0:T(8,128)(2,1)S(1)} %get-tuple-element.26), channel_id=1, source_target_pairs={{0,4},{4,8},{8,12},{12,0},{1,5},{5,9},{9,13},{13,1},{2,6},{6,10},{... | collective-permute-start | bytes 313352 | tf_op jit(solution)/shard_map/ppermute | solution.py:233
  26.8 1.6 %copy-start.2 = (bf16[16,256,256]{2,1,0:T(8,128)(2,1)S(1)}, bf16[16,256,256]{2,1,0:T(8,128)(2,1)}, u32[]{:S(2)}) copy-start(bf16[16,256,256]{2,1,0:T(8,128)(2,1)} %v_ref.1) | copy-start | bytes 6291460
  28.4 0.9 %copy-start.4 = (bf16[16,3,2048]{2,0,1:T(8,128)(2,1)S(1)}, bf16[16,3,2048]{2,0,1:T(8,128)(2,1)}, u32[]{:S(2)}) copy-start(bf16[16,3,2048]{2,0,1:T(8,128)(2,1)} %param.10) | copy-start | bytes 589828
  29.4 0.7 %copy-start.5 = (bf16[16,3,256]{2,0,1:T(8,128)(2,1)S(1)}, bf16[16,3,256]{2,0,1:T(8,128)(2,1)}, u32[]{:S(2)}) copy-start(bf16[16,3,256]{2,0,1:T(8,128)(2,1)} %param.17) | copy-start | bytes 73732
  30.1 0.7 %copy-start.6 = (bf16[16,3,256]{2,0,1:T(8,128)(2,1)S(1)}, bf16[16,3,256]{2,0,1:T(8,128)(2,1)}, u32[]{:S(2)}) copy-start(bf16[16,3,256]{2,0,1:T(8,128)(2,1)} %param.18) | copy-start | bytes 73732
  30.8 0.7 copy-start.9
  31.5 4.7 %copy-start.8 = (s32[16,1]{0,1:T(1,128)S(1)}, s32[16,1]{0,1:T(1,128)}, u32[]{:S(2)}) copy-start(s32[16,1]{0,1:T(1,128)} %param.11) | copy-start | bytes 196
  37.3 7.1 %collective-permute-start.8 = (bf16[3,16,2048]{2,1,0:T(8,128)(2,1)S(1)}, bf16[3,16,2048]{2,1,0:T(8,128)(2,1)S(1)}, u32[]{:S(2)}, u32[]{:S(2)}) collective-permute-start(bf16[3,16,2048]{2,1,0:T(8,128)(2,1)S(1)} %merge.1.refs_0_), channel_id=1, source_target_pairs={{0,12},{4,0},{8,4},{12,8},{1,13},{5,1},{9,5},{13,9},{2,14},{6,2},{... | collective-permute-start | bytes 589832 | tf_op jit(solution)/shard_map/ppermute | solution.py:233
  38.7 17.0 %collective-permute-start.7 = (bf16[3,16,2048]{2,1,0:T(8,128)(2,1)S(1)}, bf16[3,16,2048]{2,1,0:T(8,128)(2,1)S(1)}, u32[]{:S(2)}, u32[]{:S(2)}) collective-permute-start(bf16[3,16,2048]{2,1,0:T(8,128)(2,1)S(1)} %merge.1.refs_0_), channel_id=1, source_target_pairs={{0,8},{4,12},{8,0},{12,4},{1,9},{5,13},{9,1},{13,5},{2,10},{6,14},... | collective-permute-start | bytes 589832 | tf_op jit(solution)/shard_map/ppermute | solution.py:233
  39.4 16.3 %collective-permute-start.6 = (bf16[3,16,2048]{2,1,0:T(8,128)(2,1)S(1)}, bf16[3,16,2048]{2,1,0:T(8,128)(2,1)S(1)}, u32[]{:S(2)}, u32[]{:S(2)}) collective-permute-start(bf16[3,16,2048]{2,1,0:T(8,128)(2,1)S(1)} %merge.1.refs_0_), channel_id=1, source_target_pairs={{0,4},{4,8},{8,12},{12,0},{1,5},{5,9},{9,13},{13,1},{2,6},{6,10},{... | collective-permute-start | bytes 589832 | tf_op jit(solution)/shard_map/ppermute | solution.py:233
  58.9 6.6 %collective-permute-start.9 = (bf16[3,16,2048]{2,1,0:T(8,128)(2,1)S(1)}, bf16[3,16,2048]{2,1,0:T(8,128)(2,1)S(1)}, u32[]{:S(2)}, u32[]{:S(2)}) collective-permute-start(bf16[3,16,2048]{2,1,0:T(8,128)(2,1)S(1)} %get-tuple-element.30), channel_id=1, source_target_pairs={{0,1},{1,2},{2,3},{3,0},{4,5},{5,6},{6,7},{7,4},{8,9},{9,10},{10,1... | collective-permute-start | bytes 589832 | tf_op jit(solution)/shard_map/ppermute | solution.py:233
  59.0 7.8 %collective-permute-start.10 = (bf16[3,16,2048]{2,1,0:T(8,128)(2,1)S(1)}, bf16[3,16,2048]{2,1,0:T(8,128)(2,1)S(1)}, u32[]{:S(2)}, u32[]{:S(2)}) collective-permute-start(bf16[3,16,2048]{2,1,0:T(8,128)(2,1)S(1)} %get-tuple-element.31), channel_id=1, source_target_pairs={{0,2},{1,3},{2,0},{3,1},{4,6},{5,7},{6,4},{7,5},{8,10},{9,11},{10,... | collective-permute-start | bytes 589832 | tf_op jit(solution)/shard_map/ppermute | solution.py:233
  60.5 8.9 %collective-permute-start.11 = (bf16[3,16,2048]{2,1,0:T(8,128)(2,1)S(1)}, bf16[3,16,2048]{2,1,0:T(8,128)(2,1)S(1)}, u32[]{:S(2)}, u32[]{:S(2)}) collective-permute-start(bf16[3,16,2048]{2,1,0:T(8,128)(2,1)S(1)} %get-tuple-element.32), channel_id=1, source_target_pairs={{0,3},{1,0},{2,1},{3,2},{4,7},{5,4},{6,5},{7,6},{8,11},{9,8},{10,9... | collective-permute-start | bytes 589832 | tf_op jit(solution)/shard_map/ppermute | solution.py:233

commit v2 on v1

v2 whole, which is shorter than its diff:
```python
import functools
import math

import jax
import jax.numpy as jnp
from jax import lax
from jax.experimental import pallas as pl
from jax.experimental.pallas import tpu as pltpu
from jax.sharding import PartitionSpec as P

HD = 128
LANES = 128
F32 = jnp.float32
BF16 = jnp.bfloat16
HIDDEN = -1e30
MIB = 1 << 20
NT = (((1,), (1,)), ((), ()))


def params(mib):
    return pltpu.CompilerParams(vmem_limit_bytes=mib * MIB)


def cost(flops, nbytes, exps=0):
    return pl.CostEstimate(flops=flops, bytes_accessed=nbytes, transcendentals=exps)


def slots(routes_ref, count, capacity, base):
    names = [routes_ref[c] for c in range(count)]
    found = []
    for c in range(count):
        rank = jnp.int32(0)
        for earlier in range(c):
            rank = rank + (names[earlier] == names[c]).astype(jnp.int32)
        found.append((names[c] ^ base) * capacity + rank)
    return found


def spread(scalars, shape, dim):
    index = lax.broadcasted_iota(jnp.int32, shape, dim)
    out = jnp.full(shape, -1, jnp.int32)
    for c, value in enumerate(scalars):
        out = jnp.where(index == c, value, out)
    return out


def pack_kernel(capacity, relative, routes_ref, q_ref, held_ref, choice_ref, *refs):
    out_refs, (names, sems) = refs[:-2], refs[-2:]
    steps, count, _ = q_ref.shape
    name_copy = pltpu.make_async_copy(routes_ref, names, sems.at[0])
    q_copy = pltpu.make_async_copy(q_ref, held_ref, sems.at[1])
    name_copy.start()
    q_copy.start()
    base = lax.axis_index("dp") if relative else 0
    name_copy.wait()
    found = slots(names, count, capacity, base)
    shape = choice_ref.shape
    choice = spread(found, shape, 0) == lax.broadcasted_iota(jnp.int32, shape, 1)
    choice_ref[...] = choice.astype(BF16)
    shape = shape[::-1]
    placement = (spread(found, shape, 1) == lax.broadcasted_iota(jnp.int32, shape, 0)).astype(BF16)
    q_copy.wait()
    for s in range(steps):
        rows = jnp.dot(placement, held_ref[s], preferred_element_type=F32)
        at = 0
        for ref in out_refs:
            ref[s] = rows[at : at + ref.shape[1]].astype(BF16)
            at += ref.shape[1]


def suffix_kernel(
    group,
    q_ref,
    len_hbm,
    k_hbm,
    v_hbm,
    nk_hbm,
    nv_hbm,
    pk_hbm,
    pv_hbm,
    o_ref,
    l_ref,
    pk_ref,
    pv_ref,
    len_ref,
    k_ref,
    v_ref,
    nk_ref,
    nv_ref,
    qs,
    ss,
    ps,
    os,
    ls,
    sems,
):
    pairs = (
        (len_hbm, len_ref),
        (k_hbm, k_ref),
        (nk_hbm, nk_ref),
        (nv_hbm, nv_ref),
        (v_hbm, v_ref),
        (pk_hbm, pk_ref),
        (pv_hbm, pv_ref),
    )
    copies = [
        pltpu.make_async_copy(source, target, sems.at[i])
        for i, (source, target) in enumerate(pairs)
    ]
    for copy in copies:
        copy.start()
    steps, count, width = q_ref.shape
    heads = width // HD // group
    cached = k_ref.shape[1]
    each = steps * group
    rows = count * each
    scale = 1.0 / math.sqrt(HD)
    to_two = scale * math.log2(math.e)
    for h in range(heads):
        for s in range(steps):
            for g in range(group):
                piece = q_ref[s, :, pl.ds((h * group + g) * HD, HD)].astype(F32)
                qs[pl.ds(h * rows + s * group + g, count, stride=each), :] = piece
    row = lax.broadcasted_iota(jnp.int32, (rows, steps * count), 0).astype(F32)
    column = lax.broadcasted_iota(jnp.int32, (rows, steps * count), 1).astype(F32)
    row_cand = jnp.floor((row + 0.5) * (1.0 / each))
    row_step = jnp.floor((row - row_cand * each + 0.5) * (1.0 / group))
    key_step = jnp.floor((column + 0.5) * (1.0 / count))
    key_cand = column - key_step * count
    visible = (row_cand == key_cand) & (key_step <= row_step)
    position = lax.broadcasted_iota(jnp.int32, (each, cached), 1)
    for copy in copies[:4]:
        copy.wait()
    for h in range(heads):
        for c in range(count):
            qc = qs[pl.ds(h * rows + c * each, each), :].astype(BF16)
            kc = k_ref[c, :, pl.ds(h * HD, HD)]
            score = lax.dot_general(qc, kc, NT, preferred_element_type=F32)
            ss[pl.ds(c * each, each), :] = jnp.where(position < len_ref[c], score, HIDDEN)
        nk = jnp.concatenate([nk_ref[t, :, pl.ds(h * HD, HD)] for t in range(steps)], 0)
        nv = jnp.concatenate([nv_ref[t, :, pl.ds(h * HD, HD)] for t in range(steps)], 0)
        fresh = lax.dot_general(
            qs[pl.ds(h * rows, rows), :].astype(BF16), nk, NT, preferred_element_type=F32
        )
        fresh = jnp.where(visible, fresh, HIDDEN)
        score = ss[...]
        peak = jnp.maximum(
            jnp.max(score, -1, keepdims=True), jnp.max(fresh, -1, keepdims=True)
        )
        weight = jnp.exp2((score - peak) * to_two)
        fresh = jnp.exp2((fresh - peak) * to_two)
        total = jnp.sum(weight, -1, keepdims=True) + jnp.sum(fresh, -1, keepdims=True)
        ps[...] = weight.astype(BF16)
        if h == 0:
            copies[4].wait()
        os[...] = jnp.dot(fresh.astype(BF16), nv, preferred_element_type=F32)
        for c in range(count):
            vc = v_ref[c, :, pl.ds(h * HD, HD)]
            pc = ps[pl.ds(c * each, each), :]
            os[pl.ds(c * each, each), :] += jnp.dot(pc, vc, preferred_element_type=F32)
        os[...] = os[...] / total
        ls[...] = jnp.broadcast_to(peak * scale + jnp.log(total), ls.shape)
        for s in range(steps):
            for g in range(group):
                at = pl.ds(s * group + g, count, stride=each)
                lanes = pl.ds((h * group + g) * HD, HD)
                o_ref[s, :, lanes] = os[at, :]
                l_ref[s, :, lanes] = ls[at, :]
    for copy in copies[5:]:
        copy.wait()


def prompt_kernel(group, q_ref, k_ref, v_ref, out_ref):
    steps, size, width = q_ref.shape
    heads = width // HD // group
    all_heads = heads * group
    scale = 1.0 / math.sqrt(HD)
    to_two = scale * math.log2(math.e)
    lane = lax.broadcasted_iota(jnp.int32, (size, LANES), 1)
    place = lax.rem(lane, all_heads)
    logs = [jnp.zeros((size, LANES), F32) for _ in range(steps)]
    for h in range(heads):
        keys = k_ref[:, pl.ds(h * HD, HD)]
        values = v_ref[:, pl.ds(h * HD, HD)]
        q = jnp.concatenate(
            [
                q_ref[s, :, pl.ds((h * group + g) * HD, HD)]
                for s in range(steps)
                for g in range(group)
            ],
            0,
        )
        score = lax.dot_general(q, keys, NT, preferred_element_type=F32)
        peak = jnp.max(score, -1, keepdims=True)
        weight = jnp.exp2((score - peak) * to_two)
        total = jnp.sum(weight, -1, keepdims=True)
        out = jnp.dot(weight.astype(BF16), values, preferred_element_type=F32) / total
        log_total = peak * scale + jnp.log(total)
        for s in range(steps):
            for g in range(group):
                at = (s * group + g) * size
                lanes = pl.ds((h * group + g) * HD, HD)
                out_ref[s, :, lanes] = out[at : at + size].astype(BF16)
                logs[s] = jnp.where(place == h * group + g, log_total[at : at + size], logs[s])
    for s in range(steps):
        high = logs[s].astype(BF16).astype(F32)
        rest = logs[s] - high
        middle = rest.astype(BF16).astype(F32)
        low = rest - middle
        terms = jnp.where(lane < all_heads, high, jnp.where(lane < 2 * all_heads, middle, low))
        out_ref[s, :, pl.ds(width, LANES)] = terms.astype(BF16)


def merge_kernel(blocks, *refs):
    choice_ref, row_refs = refs[0], refs[1 : 1 + blocks]
    own_ref, log_ref, out_ref = refs[1 + blocks :]
    steps, count, width = own_ref.shape
    all_heads = width // HD
    choice = choice_ref[...]
    for s in range(steps):
        rows = jnp.concatenate([ref[s] for ref in row_refs], 0)
        rows = jnp.dot(choice, rows, preferred_element_type=F32)
        terms = rows[:, width:]
        logs = (
            terms[:, :all_heads]
            + terms[:, all_heads : 2 * all_heads]
            + terms[:, 2 * all_heads : 3 * all_heads]
        )
        for h in range(all_heads):
            lanes = slice(h * HD, (h + 1) * HD)
            first = jnp.broadcast_to(logs[:, h : h + 1], (count, HD))
            second = log_ref[s, :, lanes]
            peak = jnp.maximum(first, second)
            first = jnp.exp(first - peak)
            second = jnp.exp(second - peak)
            mixed = (first * rows[:, lanes] + second * own_ref[s, :, lanes]) / (first + second)
            out_ref[s, :, lanes] = mixed.astype(BF16)


def project_kernel(owners, parts, *refs):
    rows_refs, w_ref, own_ref, send_refs, held = (
        refs[:owners],
        refs[owners],
        refs[owners + 1],
        refs[owners + 2 : -1],
        refs[-1],
    )
    steps, count, _ = rows_refs[0].shape
    each = steps * count

    @pl.when(pl.program_id(0) == 0)
    def _():
        me, mine = lax.axis_index("dp"), lax.axis_index("kv")
        for shift, ref in enumerate(rows_refs):
            place = (me ^ shift) ^ mine
            for s in range(steps):
                held[place, pl.ds(s * count, count), :] = ref[s]

    product = jnp.dot(
        held[...].reshape(parts * each, held.shape[2]), w_ref[...], preferred_element_type=F32
    )
    for part, ref in enumerate((own_ref, *send_refs)):
        for s in range(steps):
            at = part * each + s * count
            ref[s] = product[at : at + count].astype(ref.dtype)


def swap(values, axis, mask):
    return lax.ppermute(values, axis, [(i, i ^ mask) for i in range(lax.axis_size(axis))])


def local(
    queries,
    routes,
    suffix_lengths,
    prefix_keys,
    prefix_values,
    suffix_keys,
    suffix_values,
    new_keys,
    new_values,
    out_weight,
):
    owners, parts = lax.axis_size("dp"), lax.axis_size("kv")
    count, steps, width = queries.shape
    kv_width = prefix_keys.shape[2]
    heads = kv_width // HD
    group = width // kv_width
    capacity = max(2, 2 * count // owners)
    direct = owners == parts == 4 and capacity % 8 == 0
    blocks = owners if direct else 1
    size = capacity if direct else owners * capacity
    vmem, hbm = pl.BlockSpec(memory_space=pltpu.VMEM), pl.BlockSpec(memory_space=pltpu.HBM)
    far = lambda values: pltpu.with_memory_space_constraint(values, pltpu.HBM)
    names = routes.reshape(count)

    q, choice, *packed = pl.pallas_call(
        functools.partial(pack_kernel, capacity, direct),
        out_shape=[
            jax.ShapeDtypeStruct((steps, count, width), BF16),
            jax.ShapeDtypeStruct((count, owners * capacity), BF16),
        ]
        + [jax.ShapeDtypeStruct((steps, size, width), BF16)] * blocks,
        in_specs=[hbm, hbm],
        out_specs=[vmem] * (blocks + 2),
        scratch_shapes=[pltpu.SMEM((count,), jnp.int32), pltpu.SemaphoreType.DMA((2,))],
        compiler_params=params(8),
        cost_estimate=cost(2 * steps * owners * capacity * count * width, 1 << 20),
        name="pack",
    )(far(names), far(queries.transpose(1, 0, 2)))

    def all_to_all(values):
        values = values.reshape(steps, owners, capacity, -1)
        moved = lax.all_to_all(values, "dp", split_axis=1, concat_axis=1, tiled=True)
        return moved.reshape(steps, owners * capacity, -1)

    if direct:
        received = [packed[0]] + [swap(packed[mask], "dp", mask) for mask in (1, 2, 3)]
    else:
        received = [all_to_all(packed[0])]

    rows = count * steps * group
    cached = suffix_keys.shape[1]
    new_shape = (steps, count, kv_width)
    own_rows, own_logs, keys, values = pl.pallas_call(
        functools.partial(suffix_kernel, group),
        out_shape=[jax.ShapeDtypeStruct((steps, count, width), F32)] * 2
        + [jax.ShapeDtypeStruct(prefix_keys.shape[1:], BF16)] * 2,
        in_specs=[vmem] + [hbm] * 7,
        out_specs=[vmem] * 4,
        scratch_shapes=[
            pltpu.SMEM((count,), jnp.int32),
            pltpu.VMEM(suffix_keys.shape, BF16),
            pltpu.VMEM(suffix_keys.shape, BF16),
            pltpu.VMEM(new_shape, BF16),
            pltpu.VMEM(new_shape, BF16),
            pltpu.VMEM((heads * rows, HD), F32),
            pltpu.VMEM((rows, cached), F32),
            pltpu.VMEM((rows, cached), BF16),
            pltpu.VMEM((rows, HD), F32),
            pltpu.VMEM((rows, LANES), F32),
            pltpu.SemaphoreType.DMA((7,)),
        ],
        compiler_params=params(16),
        cost_estimate=cost(3_000_000_000, suffix_keys.size * 4, rows * 512),
        name="suffix",
    )(
        q,
        far(suffix_lengths),
        far(suffix_keys),
        far(suffix_values),
        far(new_keys.transpose(1, 0, 2)),
        far(new_values.transpose(1, 0, 2)),
        far(prefix_keys[0]),
        far(prefix_values[0]),
    )

    prompt = pl.pallas_call(
        functools.partial(prompt_kernel, group),
        out_shape=jax.ShapeDtypeStruct((steps, size, width + LANES), BF16),
        in_specs=[vmem] * 3,
        out_specs=vmem,
        compiler_params=params(12 if direct else 48),
        cost_estimate=cost(4 * size * steps * width * prefix_keys.shape[1], prefix_keys.size * 4),
        name="prompt",
    )
    answers = [prompt(block, keys, values) for block in received]
    if direct:
        home = [answers[0]] + [swap(answers[mask], "dp", mask) for mask in (1, 2, 3)]
    else:
        home = [all_to_all(answers[0])]

    attended = pl.pallas_call(
        functools.partial(merge_kernel, blocks),
        out_shape=jax.ShapeDtypeStruct((steps, count, width), BF16),
        in_specs=[vmem] * (blocks + 3),
        out_specs=vmem,
        compiler_params=params(8),
        cost_estimate=cost(2 * steps * owners * capacity * count * width, 2 << 20),
        name="merge",
    )(choice, *home, own_rows, own_logs)

    columns = out_weight.shape[1]
    if not direct:
        block_rows = lax.all_gather(attended, "dp", axis=1, tiled=True)
        product = jnp.dot(
            block_rows.reshape(-1, width), out_weight, preferred_element_type=F32
        ).reshape(steps, -1, columns)
        total = lax.psum_scatter(product, "kv", scatter_dimension=1, tiled=True)
        return total.astype(BF16).transpose(1, 0, 2)

    gathered = [attended] + [swap(attended, "dp", mask) for mask in (1, 2, 3)]
    chunk = columns // 4
    own_sum, *sent = pl.pallas_call(
        functools.partial(project_kernel, owners, parts),
        grid=(columns // chunk,),
        out_shape=[jax.ShapeDtypeStruct((steps, count, columns), F32)]
        + [jax.ShapeDtypeStruct((steps, count, columns), BF16)] * (parts - 1),
        in_specs=[pl.BlockSpec((steps, count, width), lambda i: (0, 0, 0))] * owners
        + [pl.BlockSpec((width, chunk), lambda i: (0, i))],
        out_specs=[pl.BlockSpec((steps, count, chunk), lambda i: (0, 0, i))] * parts,
        scratch_shapes=[pltpu.VMEM((parts, steps * count, width), BF16)],
        compiler_params=params(24),
        cost_estimate=cost(2 * owners * steps * count * width * columns, out_weight.size * 2),
        name="project",
    )(*gathered, out_weight)
    total = own_sum
    for shift, values in enumerate(sent, 1):
        total = total + swap(values, "kv", shift).astype(F32)
    return total.astype(BF16).transpose(1, 0, 2)


def solution(mesh):
    placed = (
        P(("groups", "dp"), None, "kv"),
        P(("groups", "dp"), None),
        P(("groups", "dp")),
        P(("groups", "dp"), None, "kv"),
        P(("groups", "dp"), None, "kv"),
        P(("groups", "dp"), None, "kv"),
        P(("groups", "dp"), None, "kv"),
        P(("groups", "dp"), None, "kv"),
        P(("groups", "dp"), None, "kv"),
        P("kv", "dp"),
    )
    return jax.shard_map(
        local,
        mesh=mesh,
        in_specs=placed,
        out_specs=P(("groups", "kv"), None, "dp"),
        check_vma=False,
    )
```

time: 70.9 us -> 59.9 us (0.84)
  local copies, waits for them, and re-layouts: 8.69 us -> 0.01 us
  waiting for transfers between devices: 30.6 us -> 28.7 us
  Pallas kernels: 12.9 us -> 14.6 us
  starting transfers between devices: 17.2 us -> 15.6 us
    unnamed x24 -> x4, local copies, waits for them, and re-layouts: 8.69 us -> 0.01 us
    ppermute x12, waiting for transfers between devices: 30.6 us -> 28.7 us  [swap(): lax.ppermute(values, axis, [(i, i ^ mask) for i in range(lax.axis_size(ax...]
    ppermute x12, starting transfers between devices: 17.2 us -> 15.6 us  [swap(): lax.ppermute(values, axis, [(i, i ^ mask) for i in range(lax.axis_size(ax...]
    pallas_call x1, Pallas kernels: 2.28 us -> 3.7 us  [local(): pl.pallas_call(functools.partial(suffix_kernel, group), out_shape=[jax.Sh...]
    pallas_call x3 -> x6, Pallas kernels: 7.36 us -> 7.72 us  [the longest x4 6.06 us: local(): answers = [prompt(block, keys, values) for block in received]]
  transfers between devices with their start and end apart: 12 -> 12, of which waited for: 8 -> 7; matrix products, arithmetic and copies ran while one was open for 0% -> 0% of each run, Pallas kernels for 3% -> 16%
where the time goes in v2:
time: 59.9 us; the launch traced here: 59.7 us
  waiting for transfers between devices  28.7 us (48%)
  starting transfers between devices  15.6 us (26%)
  Pallas kernels  14.6 us (24%)
  other arithmetic  0.77 us (1%)
    ppermute x12, waiting for transfers between devices, swap(): lax.ppermute(values, axis, [(i, i ^ mask) for i in range(lax.axis_size(ax...  28.7 us
    ppermute x12, starting transfers between devices, swap(): lax.ppermute(values, axis, [(i, i ^ mask) for i in range(lax.axis_size(ax...  15.6 us
    pallas_call x4, Pallas kernels, local(): answers = [prompt(block, keys, values) for block in received]  6.06 us
    pallas_call x1, Pallas kernels, local(): pl.pallas_call(functools.partial(suffix_kernel, group), out_shape=[jax.Sh...  3.7 us
    pallas_call x1, Pallas kernels, local(): pl.pallas_call(functools.partial(project_kernel, owners, parts), grid=(co...  3.19 us
  transfers between devices with their start and end apart: 12, of which 7 were waited for; matrix products, arithmetic and copies ran while one was open for 0% of the time, Pallas kernels for 16%

profile of v2, /device:TPU:0, one launch (start us, length us, event | category | flops | bytes accessed | tf_op | source)
XLA Modules:
  0.0 59.7 jit_solution(13473881718564443493)
XLA Ops:
  0.0 1.2 %pack.1 = (bf16[3,16,2048]{2,1,0:T(8,128)(2,1)S(1)}, bf16[16,32]{1,0:T(8,128)(2,1)S(1)}, bf16[3,8,2048]{2,1,0:T(8,128)(2,1)S(1)}, bf16[3,8,2048]{2,1,0:T(8,128)(...) custom-call(s32[16]{0:T(128)} %bitcast.11, bf16[3,16,2048]{2,1,0:T(8,128)(2,1)} %bitcast.10), custom_call_target="tpu_custom_call" | custom-call | flops 6291456 | bytes 1048576 | tf_op jit(solution)/shard_map/pack/pallas_call | solution.py:297
  1.2 3.1 %collective-permute-start = (bf16[3,8,2048]{2,1,0:T(8,128)(2,1)S(1)}, bf16[3,8,2048]{2,1,0:T(8,128)(2,1)S(1)}, u32[]{:S(2)}, u32[]{:S(2)}) collective-permute-start(bf16[3,8,2048]{2,1,0:T(8,128)(2,1)S(1)} %get-tuple-element.24), channel_id=1, source_target_pairs={{0,4},{4,0},{8,12},{12,8},{1,5},{5,1},{9,13},{13,9},{2,6},{6,2},{1... | collective-permute-start | bytes 294920 | tf_op jit(solution)/shard_map/ppermute | solution.py:269
  4.3 2.6 %collective-permute-start.2 = (bf16[3,8,2048]{2,1,0:T(8,128)(2,1)S(1)}, bf16[3,8,2048]{2,1,0:T(8,128)(2,1)S(1)}, u32[]{:S(2)}, u32[]{:S(2)}) collective-permute-start(bf16[3,8,2048]{2,1,0:T(8,128)(2,1)S(1)} %get-tuple-element.25), channel_id=1, source_target_pairs={{0,8},{4,12},{8,0},{12,4},{1,9},{5,13},{9,1},{13,5},{2,10},{6,14},... | collective-permute-start | bytes 294920 | tf_op jit(solution)/shard_map/ppermute | solution.py:269
  6.9 0.0 collective-permute-start.4
  6.9 0.0 slice-start
  6.9 0.0 slice-start.1
  6.9 3.7 %suffix.1 = (f32[3,16,2048]{2,1,0:T(8,128)S(1)}, f32[3,16,2048]{2,1,0:T(8,128)S(1)}, bf16[2048,256]{1,0:T(8,128)(2,1)S(1)}, bf16[2048,256]{1,0:T(8,128)(2,1)S(1)}) custom-call(bf16[3,16,2048]{2,1,0:T(8,128)(2,1)S(1)} %get-tuple-element.21.q_ref, s32[16]{0:T(128)} %len_hbm.1, bf16[16,256,256]{2,1,0:T(8,128)(2,1)} %k_hbm.1, bf16[16,256,256]{2,1,0:T(8,128)(2,1)} %v_hbm.1, ...), custom_call_target="tpu_custom_call" | custom-call | flops 3000000000 | bytes 4194304 | tf_op jit(solution)/shard_map/suffix/pallas_call | solution.py:325
  10.6 0.0 collective-permute-done.q_ref
  10.6 1.5 %prompt.5 = bf16[3,8,2176]{2,1,0:T(8,128)(2,1)S(1)} custom-call(bf16[3,8,2048]{2,1,0:T(8,128)(2,1)S(1)} %collective-permute-done.q_ref, bf16[2048,256]{1,0:T(8,128)(2,1)S(1)} %get-tuple-element.22.k_ref, bf16[2048,256]{1,0:T(8,128)(2,1)S(1)} %get-tuple-element.23.v_ref), custom_call_target="tpu_custom_call" | custom-call | flops 402653184 | bytes 2097152 | tf_op jit(solution)/shard_map/prompt/pallas_call | solution.py:367
  12.1 1.0 %collective-permute-start.1 = (bf16[3,8,2176]{2,1,0:T(8,128)(2,1)S(1)}, bf16[3,8,2176]{2,1,0:T(8,128)(2,1)S(1)}, u32[]{:S(2)}, u32[]{:S(2)}) collective-permute-start(bf16[3,8,2176]{2,1,0:T(8,128)(2,1)S(1)} %prompt.5), channel_id=1, source_target_pairs={{0,4},{4,0},{8,12},{12,8},{1,5},{5,1},{9,13},{13,9},{2,6},{6,2},{1... | collective-permute-start | bytes 313352 | tf_op jit(solution)/shard_map/ppermute | solution.py:269
  13.1 1.7 %collective-permute-done.2.q_ref = bf16[3,8,2048]{2,1,0:T(8,128)(2,1)S(1)} collective-permute-done((bf16[3,8,2048]{2,1,0:T(8,128)(2,1)S(1)}, bf16[3,8,2048]{2,1,0:T(8,128)(2,1)S(1)}, u32[]{:S(2)}, u32[]{:S(2)}) %collective-permute-start.2) | collective-permute-done | bytes 98336 | tf_op jit(solution)/shard_map/ppermute | solution.py:269
  14.8 1.5 %prompt.6 = bf16[3,8,2176]{2,1,0:T(8,128)(2,1)S(1)} custom-call(bf16[3,8,2048]{2,1,0:T(8,128)(2,1)S(1)} %collective-permute-done.2.q_ref, bf16[2048,256]{1,0:T(8,128)(2,1)S(1)} %get-tuple-element.22.k_ref, bf16[2048,256]{1,0:T(8,128)(2,1)S(1)} %get-tuple-element.23.v_ref), custom_call_target="tpu_custom_call" | custom-call | flops 402653184 | bytes 2097152 | tf_op jit(solution)/shard_map/prompt/pallas_call | solution.py:367
  16.3 1.8 %collective-permute-start.3 = (bf16[3,8,2176]{2,1,0:T(8,128)(2,1)S(1)}, bf16[3,8,2176]{2,1,0:T(8,128)(2,1)S(1)}, u32[]{:S(2)}, u32[]{:S(2)}) collective-permute-start(bf16[3,8,2176]{2,1,0:T(8,128)(2,1)S(1)} %prompt.6), channel_id=1, source_target_pairs={{0,8},{4,12},{8,0},{12,4},{1,9},{5,13},{9,1},{13,5},{2,10},{6,14},... | collective-permute-start | bytes 313352 | tf_op jit(solution)/shard_map/ppermute | solution.py:269
  18.2 0.0 collective-permute-done.4.q_ref
  18.2 1.5 %prompt.7 = bf16[3,8,2176]{2,1,0:T(8,128)(2,1)S(1)} custom-call(bf16[3,8,2048]{2,1,0:T(8,128)(2,1)S(1)} %collective-permute-done.4.q_ref, bf16[2048,256]{1,0:T(8,128)(2,1)S(1)} %get-tuple-element.22.k_ref, bf16[2048,256]{1,0:T(8,128)(2,1)S(1)} %get-tuple-element.23.v_ref), custom_call_target="tpu_custom_call" | custom-call | flops 402653184 | bytes 2097152 | tf_op jit(solution)/shard_map/prompt/pallas_call | solution.py:367
  19.7 0.7 %collective-permute-start.5 = (bf16[3,8,2176]{2,1,0:T(8,128)(2,1)S(1)}, bf16[3,8,2176]{2,1,0:T(8,128)(2,1)S(1)}, u32[]{:S(2)}, u32[]{:S(2)}) collective-permute-start(bf16[3,8,2176]{2,1,0:T(8,128)(2,1)S(1)} %prompt.7), channel_id=1, source_target_pairs={{0,12},{4,8},{8,4},{12,0},{1,13},{5,9},{9,5},{13,1},{2,14},{6,10},... | collective-permute-start | bytes 313352 | tf_op jit(solution)/shard_map/ppermute | solution.py:269
  20.4 1.5 %prompt.4.refs_1_ = bf16[3,8,2176]{2,1,0:T(8,128)(2,1)S(1)} custom-call(bf16[3,8,2048]{2,1,0:T(8,128)(2,1)S(1)} %get-tuple-element.20.q_ref, bf16[2048,256]{1,0:T(8,128)(2,1)S(1)} %get-tuple-element.22.k_ref, bf16[2048,256]{1,0:T(8,128)(2,1)S(1)} %get-tuple-element.23.v_ref), custom_call_target="tpu_custom_call" | custom-call | flops 402653184 | bytes 2097152 | tf_op jit(solution)/shard_map/prompt/pallas_call | solution.py:367
  21.9 0.0 collective-permute-done.1.refs_2_
  21.9 2.9 %collective-permute-done.3.refs_3_ = bf16[3,8,2176]{2,1,0:T(8,128)(2,1)S(1)} collective-permute-done((bf16[3,8,2176]{2,1,0:T(8,128)(2,1)S(1)}, bf16[3,8,2176]{2,1,0:T(8,128)(2,1)S(1)}, u32[]{:S(2)}, u32[]{:S(2)}) %collective-permute-start.3) | collective-permute-done | bytes 104480 | tf_op jit(solution)/shard_map/ppermute | solution.py:269
  24.8 1.5 %collective-permute-done.5.refs_4_ = bf16[3,8,2176]{2,1,0:T(8,128)(2,1)S(1)} collective-permute-done((bf16[3,8,2176]{2,1,0:T(8,128)(2,1)S(1)}, bf16[3,8,2176]{2,1,0:T(8,128)(2,1)S(1)}, u32[]{:S(2)}, u32[]{:S(2)}) %collective-permute-start.5) | collective-permute-done | bytes 104480 | tf_op jit(solution)/shard_map/ppermute | solution.py:269
  26.3 0.5 merge.1.refs_0_
  26.8 1.7 %collective-permute-start.8 = (bf16[3,16,2048]{2,1,0:T(8,128)(2,1)S(1)}, bf16[3,16,2048]{2,1,0:T(8,128)(2,1)S(1)}, u32[]{:S(2)}, u32[]{:S(2)}) collective-permute-start(bf16[3,16,2048]{2,1,0:T(8,128)(2,1)S(1)} %merge.1.refs_0_), channel_id=1, source_target_pairs={{0,12},{4,8},{8,4},{12,0},{1,13},{5,9},{9,5},{13,1},{2,14},{6,10},... | collective-permute-start | bytes 589832 | tf_op jit(solution)/shard_map/ppermute | solution.py:269
  28.6 1.1 %collective-permute-start.7 = (bf16[3,16,2048]{2,1,0:T(8,128)(2,1)S(1)}, bf16[3,16,2048]{2,1,0:T(8,128)(2,1)S(1)}, u32[]{:S(2)}, u32[]{:S(2)}) collective-permute-start(bf16[3,16,2048]{2,1,0:T(8,128)(2,1)S(1)} %merge.1.refs_0_), channel_id=1, source_target_pairs={{0,8},{4,12},{8,0},{12,4},{1,9},{5,13},{9,1},{13,5},{2,10},{6,14},... | collective-permute-start | bytes 589832 | tf_op jit(solution)/shard_map/ppermute | solution.py:269
  29.6 1.7 %collective-permute-start.6 = (bf16[3,16,2048]{2,1,0:T(8,128)(2,1)S(1)}, bf16[3,16,2048]{2,1,0:T(8,128)(2,1)S(1)}, u32[]{:S(2)}, u32[]{:S(2)}) collective-permute-start(bf16[3,16,2048]{2,1,0:T(8,128)(2,1)S(1)} %merge.1.refs_0_), channel_id=1, source_target_pairs={{0,4},{4,0},{8,12},{12,8},{1,5},{5,1},{9,13},{13,9},{2,6},{6,2},{1... | collective-permute-start | bytes 589832 | tf_op jit(solution)/shard_map/ppermute | solution.py:269
  31.3 5.2 %collective-permute-done.8.refs_3_ = bf16[3,16,2048]{2,1,0:T(8,128)(2,1)S(1)} collective-permute-done((bf16[3,16,2048]{2,1,0:T(8,128)(2,1)S(1)}, bf16[3,16,2048]{2,1,0:T(8,128)(2,1)S(1)}, u32[]{:S(2)}, u32[]{:S(2)}) %collective-permute-start.8) | collective-permute-done | bytes 196640 | tf_op jit(solution)/shard_map/ppermute | solution.py:269
  36.5 8.2 %collective-permute-done.7.refs_2_ = bf16[3,16,2048]{2,1,0:T(8,128)(2,1)S(1)} collective-permute-done((bf16[3,16,2048]{2,1,0:T(8,128)(2,1)S(1)}, bf16[3,16,2048]{2,1,0:T(8,128)(2,1)S(1)}, u32[]{:S(2)}, u32[]{:S(2)}) %collective-permute-start.7) | collective-permute-done | bytes 196640 | tf_op jit(solution)/shard_map/ppermute | solution.py:269
  44.7 0.0 collective-permute-done.6.refs_1_
  44.7 0.0 slice-done
  44.7 0.0 slice-done.1
  44.7 3.2 %project.1 = (f32[3,16,2048]{2,1,0:T(8,128)S(1)}, bf16[3,16,2048]{2,1,0:T(8,128)(2,1)S(1)}, bf16[3,16,2048]{2,1,0:T(8,128)(2,1)S(1)}, bf16[3,16,2048]{2,1,0:T(8,128)(2,1)S(1)}) custom-call(bf16[3,16,2048]{2,1,0:T(8,128)(2,1)S(1)} %merge.1.refs_0_, bf16[3,16,2048]{2,1,0:T(8,128)(2,1)S(1)} %collective-permute-done.6.refs_1_, ...), custom_call_target="tpu_custom_call" | custom-call | flops 1610612736 | bytes 8388608 | tf_op jit(solution)/shard_map/project/pallas_call | solution.py:394
  47.9 0.1 collective-permute-start.9
  48.0 1.5 %collective-permute-start.10 = (bf16[3,16,2048]{2,1,0:T(8,128)(2,1)S(1)}, bf16[3,16,2048]{2,1,0:T(8,128)(2,1)S(1)}, u32[]{:S(2)}, u32[]{:S(2)}) collective-permute-start(bf16[3,16,2048]{2,1,0:T(8,128)(2,1)S(1)} %get-tuple-element.31), channel_id=1, source_target_pairs={{0,2},{1,3},{2,0},{3,1},{4,6},{5,7},{6,4},{7,5},{8,10},{9,11},{10,... | collective-permute-start | bytes 589832 | tf_op jit(solution)/shard_map/ppermute | solution.py:269
  49.6 0.3 collective-permute-start.11
  49.9 0.0 collective-permute-done.9
  49.9 6.0 %collective-permute-done.10 = bf16[3,16,2048]{2,1,0:T(8,128)(2,1)S(1)} collective-permute-done((bf16[3,16,2048]{2,1,0:T(8,128)(2,1)S(1)}, bf16[3,16,2048]{2,1,0:T(8,128)(2,1)S(1)}, u32[]{:S(2)}, u32[]{:S(2)}) %collective-permute-start.10) | collective-permute-done | bytes 196640 | tf_op jit(solution)/shard_map/ppermute | solution.py:269
  55.9 3.1 %collective-permute-done.11 = bf16[3,16,2048]{2,1,0:T(8,128)(2,1)S(1)} collective-permute-done((bf16[3,16,2048]{2,1,0:T(8,128)(2,1)S(1)}, bf16[3,16,2048]{2,1,0:T(8,128)(2,1)S(1)}, u32[]{:S(2)}, u32[]{:S(2)}) %collective-permute-start.11) | collective-permute-done | bytes 196640 | tf_op jit(solution)/shard_map/ppermute | solution.py:269
  59.0 0.8 %fusion = bf16[16,3,2048]{2,0,1:T(8,128)(2,1)} fusion(bf16[3,16,2048]{2,1,0:T(8,128)(2,1)S(1)} %collective-permute-done.11, bf16[3,16,2048]{2,1,0:T(8,128)(2,1)S(1)} %collective-permute-done.10, f32[3,16,2048]{2,1,0:T(8,128)S(1)} %get-tuple-element.29, bf16[3,16,2048]{2,1,0:T(8,128)(2,1)S(1)} %collective-permute-done.9), kind=kLoop, calls=%fused_computation.1 | loop fusion | flops 688128 | bytes 1179648 | tf_op jit(solution)/shard_map/transpose | solution.py:410
  (1 shorter events, 0.0 us)
Async XLA Ops:
  1.2 9.4 %collective-permute-start = (bf16[3,8,2048]{2,1,0:T(8,128)(2,1)S(1)}, bf16[3,8,2048]{2,1,0:T(8,128)(2,1)S(1)}, u32[]{:S(2)}, u32[]{:S(2)}) collective-permute-start(bf16[3,8,2048]{2,1,0:T(8,128)(2,1)S(1)} %get-tuple-element.24), channel_id=1, source_target_pairs={{0,4},{4,0},{8,12},{12,8},{1,5},{5,1},{9,13},{13,9},{2,6},{6,2},{1... | collective-permute-start | bytes 294920 | tf_op jit(solution)/shard_map/ppermute | solution.py:269
  4.3 10.5 %collective-permute-start.2 = (bf16[3,8,2048]{2,1,0:T(8,128)(2,1)S(1)}, bf16[3,8,2048]{2,1,0:T(8,128)(2,1)S(1)}, u32[]{:S(2)}, u32[]{:S(2)}) collective-permute-start(bf16[3,8,2048]{2,1,0:T(8,128)(2,1)S(1)} %get-tuple-element.25), channel_id=1, source_target_pairs={{0,8},{4,12},{8,0},{12,4},{1,9},{5,13},{9,1},{13,5},{2,10},{6,14},... | collective-permute-start | bytes 294920 | tf_op jit(solution)/shard_map/ppermute | solution.py:269
  6.9 11.3 %collective-permute-start.4 = (bf16[3,8,2048]{2,1,0:T(8,128)(2,1)S(1)}, bf16[3,8,2048]{2,1,0:T(8,128)(2,1)S(1)}, u32[]{:S(2)}, u32[]{:S(2)}) collective-permute-start(bf16[3,8,2048]{2,1,0:T(8,128)(2,1)S(1)} %get-tuple-element.26), channel_id=1, source_target_pairs={{0,12},{4,8},{8,4},{12,0},{1,13},{5,9},{9,5},{13,1},{2,14},{6,10},... | collective-permute-start | bytes 294920 | tf_op jit(solution)/shard_map/ppermute | solution.py:269
  6.9 37.8 %slice-start = ((s8[8388608]{0:T(1024)(128)(4,1)}), s8[4194304]{0:T(1024)(128)(4,1)S(1)}, s32[]{:S(2)}) async-start(s8[8388608]{0:T(1024)(128)(4,1)} %bitcast.8), calls=%async_computation | async-start | bytes 8388608
  6.9 37.8 %slice-start.1 = ((s8[8388608]{0:T(1024)(128)(4,1)}), s8[4194304]{0:T(1024)(128)(4,1)S(1)}, s32[]{:S(2)}) async-start(s8[8388608]{0:T(1024)(128)(4,1)} %bitcast.8), calls=%async_computation.1 | async-start | bytes 8388608
  12.1 9.8 %collective-permute-start.1 = (bf16[3,8,2176]{2,1,0:T(8,128)(2,1)S(1)}, bf16[3,8,2176]{2,1,0:T(8,128)(2,1)S(1)}, u32[]{:S(2)}, u32[]{:S(2)}) collective-permute-start(bf16[3,8,2176]{2,1,0:T(8,128)(2,1)S(1)} %prompt.5), channel_id=1, source_target_pairs={{0,4},{4,0},{8,12},{12,8},{1,5},{5,1},{9,13},{13,9},{2,6},{6,2},{1... | collective-permute-start | bytes 313352 | tf_op jit(solution)/shard_map/ppermute | solution.py:269
  16.3 8.5 %collective-permute-start.3 = (bf16[3,8,2176]{2,1,0:T(8,128)(2,1)S(1)}, bf16[3,8,2176]{2,1,0:T(8,128)(2,1)S(1)}, u32[]{:S(2)}, u32[]{:S(2)}) collective-permute-start(bf16[3,8,2176]{2,1,0:T(8,128)(2,1)S(1)} %prompt.6), channel_id=1, source_target_pairs={{0,8},{4,12},{8,0},{12,4},{1,9},{5,13},{9,1},{13,5},{2,10},{6,14},... | collective-permute-start | bytes 313352 | tf_op jit(solution)/shard_map/ppermute | solution.py:269
  19.7 6.6 %collective-permute-start.5 = (bf16[3,8,2176]{2,1,0:T(8,128)(2,1)S(1)}, bf16[3,8,2176]{2,1,0:T(8,128)(2,1)S(1)}, u32[]{:S(2)}, u32[]{:S(2)}) collective-permute-start(bf16[3,8,2176]{2,1,0:T(8,128)(2,1)S(1)} %prompt.7), channel_id=1, source_target_pairs={{0,12},{4,8},{8,4},{12,0},{1,13},{5,9},{9,5},{13,1},{2,14},{6,10},... | collective-permute-start | bytes 313352 | tf_op jit(solution)/shard_map/ppermute | solution.py:269
  26.8 9.6 %collective-permute-start.8 = (bf16[3,16,2048]{2,1,0:T(8,128)(2,1)S(1)}, bf16[3,16,2048]{2,1,0:T(8,128)(2,1)S(1)}, u32[]{:S(2)}, u32[]{:S(2)}) collective-permute-start(bf16[3,16,2048]{2,1,0:T(8,128)(2,1)S(1)} %merge.1.refs_0_), channel_id=1, source_target_pairs={{0,12},{4,8},{8,4},{12,0},{1,13},{5,9},{9,5},{13,1},{2,14},{6,10},... | collective-permute-start | bytes 589832 | tf_op jit(solution)/shard_map/ppermute | solution.py:269
  28.6 16.1 %collective-permute-start.7 = (bf16[3,16,2048]{2,1,0:T(8,128)(2,1)S(1)}, bf16[3,16,2048]{2,1,0:T(8,128)(2,1)S(1)}, u32[]{:S(2)}, u32[]{:S(2)}) collective-permute-start(bf16[3,16,2048]{2,1,0:T(8,128)(2,1)S(1)} %merge.1.refs_0_), channel_id=1, source_target_pairs={{0,8},{4,12},{8,0},{12,4},{1,9},{5,13},{9,1},{13,5},{2,10},{6,14},... | collective-permute-start | bytes 589832 | tf_op jit(solution)/shard_map/ppermute | solution.py:269
  29.6 15.1 %collective-permute-start.6 = (bf16[3,16,2048]{2,1,0:T(8,128)(2,1)S(1)}, bf16[3,16,2048]{2,1,0:T(8,128)(2,1)S(1)}, u32[]{:S(2)}, u32[]{:S(2)}) collective-permute-start(bf16[3,16,2048]{2,1,0:T(8,128)(2,1)S(1)} %merge.1.refs_0_), channel_id=1, source_target_pairs={{0,4},{4,0},{8,12},{12,8},{1,5},{5,1},{9,13},{13,9},{2,6},{6,2},{1... | collective-permute-start | bytes 589832 | tf_op jit(solution)/shard_map/ppermute | solution.py:269
  47.9 1.9 %collective-permute-start.9 = (bf16[3,16,2048]{2,1,0:T(8,128)(2,1)S(1)}, bf16[3,16,2048]{2,1,0:T(8,128)(2,1)S(1)}, u32[]{:S(2)}, u32[]{:S(2)}) collective-permute-start(bf16[3,16,2048]{2,1,0:T(8,128)(2,1)S(1)} %get-tuple-element.30), channel_id=1, source_target_pairs={{0,1},{1,0},{2,3},{3,2},{4,5},{5,4},{6,7},{7,6},{8,9},{9,8},{10,11... | collective-permute-start | bytes 589832 | tf_op jit(solution)/shard_map/ppermute | solution.py:269
  48.0 7.8 %collective-permute-start.10 = (bf16[3,16,2048]{2,1,0:T(8,128)(2,1)S(1)}, bf16[3,16,2048]{2,1,0:T(8,128)(2,1)S(1)}, u32[]{:S(2)}, u32[]{:S(2)}) collective-permute-start(bf16[3,16,2048]{2,1,0:T(8,128)(2,1)S(1)} %get-tuple-element.31), channel_id=1, source_target_pairs={{0,2},{1,3},{2,0},{3,1},{4,6},{5,7},{6,4},{7,5},{8,10},{9,11},{10,... | collective-permute-start | bytes 589832 | tf_op jit(solution)/shard_map/ppermute | solution.py:269
  49.6 9.4 %collective-permute-start.11 = (bf16[3,16,2048]{2,1,0:T(8,128)(2,1)S(1)}, bf16[3,16,2048]{2,1,0:T(8,128)(2,1)S(1)}, u32[]{:S(2)}, u32[]{:S(2)}) collective-permute-start(bf16[3,16,2048]{2,1,0:T(8,128)(2,1)S(1)} %get-tuple-element.32), channel_id=1, source_target_pairs={{0,3},{1,2},{2,1},{3,0},{4,7},{5,6},{6,5},{7,4},{8,11},{9,10},{10,... | collective-permute-start | bytes 589832 | tf_op jit(solution)/shard_map/ppermute | solution.py:269

commit v3 on v2

--- a/solution.py
+++ b/solution.py
@@ -7,6 +7,7 @@
 from jax.experimental import pallas as pl
 from jax.experimental.pallas import tpu as pltpu
 from jax.sharding import PartitionSpec as P
+
 
 HD = 128
 LANES = 128
@@ -237,36 +238,52 @@
             out_ref[s, :, lanes] = mixed.astype(BF16)
 
 
-def project_kernel(owners, parts, *refs):
-    rows_refs, w_ref, own_ref, send_refs, held = (
-        refs[:owners],
-        refs[owners],
-        refs[owners + 1],
-        refs[owners + 2 : -1],
-        refs[-1],
-    )
-    steps, count, _ = rows_refs[0].shape
+def project_kernel(shifts, *refs):
+    *rows_refs, w_ref, keep_ref, send_ref, held = refs
+    steps, count, _ = keep_ref.shape
     each = steps * count
 
     @pl.when(pl.program_id(0) == 0)
     def _():
         me, mine = lax.axis_index("dp"), lax.axis_index("kv")
-        for shift, ref in enumerate(rows_refs):
-            place = (me ^ shift) ^ mine
-            for s in range(steps):
-                held[place, pl.ds(s * count, count), :] = ref[s]
+        inner = (me == 1) | (me == 2)
+        for at, shift in enumerate(shifts):
+            place = ((me ^ shift) ^ mine) & 1
+            choices = rows_refs[2 * at : 2 * at + 2] if len(rows_refs) > 2 else rows_refs[at:at + 1]
+            if len(choices) == 1:
+                for s in range(steps):
+                    held[place, pl.ds(s * count, count), :] = choices[0][s]
+            else:
+
+                @pl.when(inner)
+                def _():
+                    for s in range(steps):
+                        held[place, pl.ds(s * count, count), :] = choices[0][s]
+
+                @pl.when(jnp.logical_not(inner))
+                def _():
+                    for s in range(steps):
+                        held[place, pl.ds(s * count, count), :] = choices[1][s]
 
     product = jnp.dot(
-        held[...].reshape(parts * each, held.shape[2]), w_ref[...], preferred_element_type=F32
-    )
-    for part, ref in enumerate((own_ref, *send_refs)):
+        held[...].reshape(2 * each, held.shape[2]), w_ref[...], preferred_element_type=F32
+    )
+    for part, ref in enumerate((keep_ref, send_ref)):
         for s in range(steps):
             at = part * each + s * count
             ref[s] = product[at : at + count].astype(ref.dtype)
 
 
+def add_kernel(keep_ref, got_ref, sum_ref, send_ref):
+    for s in range(keep_ref.shape[0]):
+        total = keep_ref[s] + got_ref[s].astype(F32)
+        sum_ref[s] = total
+        send_ref[s] = total.astype(BF16)
+
+
 def swap(values, axis, mask):
-    return lax.ppermute(values, axis, [(i, i ^ mask) for i in range(lax.axis_size(axis))])
+    pairs = [(i, i ^ mask) for i in range(lax.axis_size(axis))]
+    return lax.ppermute(values, axis, pairs)
 
 
 def local(
@@ -315,7 +332,7 @@
         return moved.reshape(steps, owners * capacity, -1)
 
     if direct:
-        received = [packed[0]] + [swap(packed[mask], "dp", mask) for mask in (1, 2, 3)]
+        received = [packed[0]] + [swap(packed[i], "dp", i) for i in (1, 2, 3)]
     else:
         received = [all_to_all(packed[0])]
 
@@ -364,9 +381,11 @@
         cost_estimate=cost(4 * size * steps * width * prefix_keys.shape[1], prefix_keys.size * 4),
         name="prompt",
     )
-    answers = [prompt(block, keys, values) for block in received]
+    answers = []
+    for asked in received:
+        answers.append(prompt(asked, keys, values))
     if direct:
-        home = [answers[0]] + [swap(answers[mask], "dp", mask) for mask in (1, 2, 3)]
+        home = [answers[0]] + [swap(answers[i], "dp", i) for i in (1, 2, 3)]
     else:
         home = [all_to_all(answers[0])]
 
@@ -389,24 +408,65 @@
         total = lax.psum_scatter(product, "kv", scatter_dimension=1, tiled=True)
         return total.astype(BF16).transpose(1, 0, 2)
 
-    gathered = [attended] + [swap(attended, "dp", mask) for mask in (1, 2, 3)]
+    def move(values, pairs):
+        return lax.ppermute(values, "dp", pairs)
+
+    def across(values, inward):
+        pairs = []
+        for d in range(owners):
+            for c in range(2):
+                here, there = 2 * (d >> 1) + c, 2 * (1 - (d >> 1)) + c
+                source, target = (there, here) if inward else (here, there)
+                pairs.append((d * parts + source, d * parts + target))
+        return lax.ppermute(values, ("dp", "kv"), pairs)
+
     chunk = columns // 4
-    own_sum, *sent = pl.pallas_call(
-        functools.partial(project_kernel, owners, parts),
-        grid=(columns // chunk,),
-        out_shape=[jax.ShapeDtypeStruct((steps, count, columns), F32)]
-        + [jax.ShapeDtypeStruct((steps, count, columns), BF16)] * (parts - 1),
-        in_specs=[pl.BlockSpec((steps, count, width), lambda i: (0, 0, 0))] * owners
-        + [pl.BlockSpec((width, chunk), lambda i: (0, i))],
-        out_specs=[pl.BlockSpec((steps, count, chunk), lambda i: (0, 0, i))] * parts,
-        scratch_shapes=[pltpu.VMEM((parts, steps * count, width), BF16)],
-        compiler_params=params(24),
-        cost_estimate=cost(2 * owners * steps * count * width * columns, out_weight.size * 2),
-        name="project",
-    )(*gathered, out_weight)
-    total = own_sum
-    for shift, values in enumerate(sent, 1):
-        total = total + swap(values, "kv", shift).astype(F32)
+    block = pl.BlockSpec((steps, count, width), lambda i: (0, 0, 0))
+    narrow = pl.BlockSpec((steps, count, chunk), lambda i: (0, 0, i))
+
+    def project(shifts, rows):
+        return pl.pallas_call(
+            functools.partial(project_kernel, shifts),
+            grid=(columns // chunk,),
+            out_shape=[
+                jax.ShapeDtypeStruct((steps, count, columns), F32),
+                jax.ShapeDtypeStruct((steps, count, columns), BF16),
+            ],
+            in_specs=[block] * len(rows) + [pl.BlockSpec((width, chunk), lambda i: (0, i))],
+            out_specs=[narrow, narrow],
+            scratch_shapes=[pltpu.VMEM((2, steps * count, width), BF16)],
+            compiler_params=params(16),
+            cost_estimate=cost(4 * steps * count * width * columns, out_weight.size * 2),
+            name="project",
+        )(*rows, out_weight)
+
+    def add(keep, got):
+        return pl.pallas_call(
+            add_kernel,
+            out_shape=[
+                jax.ShapeDtypeStruct(keep.shape, F32),
+                jax.ShapeDtypeStruct(keep.shape, BF16),
+            ],
+            in_specs=[vmem] * 2,
+            out_specs=[vmem] * 2,
+            compiler_params=params(4),
+            cost_estimate=cost(keep.size, keep.size * 12),
+            name="add",
+        )(keep, got)
+
+    beside = swap(attended, "dp", 1)
+    middle = move(attended, [(1, 2), (2, 1)])
+    far_in = move(attended, [(0, 2), (3, 1)])
+    passed = move(middle, [(2, 3), (1, 0)])
+    passed_far = move(far_in, [(2, 3), (1, 0)])
+    near_keep, near_send = project((0, 1), [attended, beside])
+    near_sum, near_send = add(near_keep, swap(near_send, "kv", 1))
+    near_in = across(near_send, True)
+    far_keep, far_send = project((2, 3), [far_in, passed, middle, passed_far])
+    far_sum, far_send = add(far_keep, swap(far_send, "kv", 1))
+    far_out = across(far_send, False)
+    mine = lax.axis_index("kv") >> 1 == lax.axis_index("dp") >> 1
+    total = jnp.where(mine, near_sum, far_sum) + near_in.astype(F32) + far_out.astype(F32)
     return total.astype(BF16).transpose(1, 0, 2)
 
 

time: 59.9 us -> 58.9 us (0.983)
  waiting for transfers between devices: 28.7 us -> 15 us
  starting transfers between devices: 15.6 us -> 25.9 us
  Pallas kernels: 14.6 us -> 16.9 us
    ppermute x12 -> x15, waiting for transfers between devices: 28.7 us -> 15 us  [the longest x4 6.13 us: move(): return lax.ppermute(values, 'dp', pairs)]
    ppermute x12 -> x15, starting transfers between devices: 15.6 us -> 25.9 us  [the longest x9 11.6 us: swap(): return lax.ppermute(values, axis, pairs)]
    pallas_call x5 -> x8, Pallas kernels: 9.25 us -> 11.5 us  [the longest x4 6.07 us: local(): answers.append(prompt(asked, keys, values))]
  transfers between devices with their start and end apart: 12 -> 15, of which waited for: 7 -> 9; matrix products, arithmetic and copies ran while one was open for 0% -> 0% of each run, Pallas kernels for 16% -> 26%
where the time goes in v3:
time: 58.9 us; the launch traced here: 58.7 us
  starting transfers between devices  25.9 us (44%)
  Pallas kernels  16.9 us (29%)
  waiting for transfers between devices  15 us (25%)
  other arithmetic  0.75 us (1%)
    ppermute x9, starting transfers between devices, swap(): return lax.ppermute(values, axis, pairs)  11.6 us
    ppermute x4, starting transfers between devices, move(): return lax.ppermute(values, 'dp', pairs)  8.48 us
    ppermute x4, waiting for transfers between devices, move(): return lax.ppermute(values, 'dp', pairs)  6.13 us
    pallas_call x4, Pallas kernels, local(): answers.append(prompt(asked, keys, values))  6.07 us
    ppermute x2, starting transfers between devices, across(): return lax.ppermute(values, ('dp', 'kv'), pairs)  5.81 us
    pallas_call x2, Pallas kernels, project(): pl.pallas_call(functools.partial(project_kernel, shifts), grid=(columns /...  5.36 us
    ppermute x2, waiting for transfers between devices, across(): return lax.ppermute(values, ('dp', 'kv'), pairs)  4.49 us
    ppermute x9, waiting for transfers between devices, swap(): return lax.ppermute(values, axis, pairs)  4.38 us
  transfers between devices with their start and end apart: 15, of which 9 were waited for; matrix products, arithmetic and copies ran while one was open for 0% of the time, Pallas kernels for 26%

profile of v3, /device:TPU:0, one launch (start us, length us, event | category | flops | bytes accessed | tf_op | source)
XLA Modules:
  0.0 58.7 jit_solution(9673209675694745284)
XLA Ops:
  0.0 1.2 %pack.1 = (bf16[3,16,2048]{2,1,0:T(8,128)(2,1)S(1)}, bf16[16,32]{1,0:T(8,128)(2,1)S(1)}, bf16[3,8,2048]{2,1,0:T(8,128)(2,1)S(1)}, bf16[3,8,2048]{2,1,0:T(8,128)(...) custom-call(s32[16]{0:T(128)} %bitcast.11, bf16[3,16,2048]{2,1,0:T(8,128)(2,1)} %bitcast.10), custom_call_target="tpu_custom_call" | custom-call | flops 6291456 | bytes 1048576 | tf_op jit(solution)/shard_map/pack/pallas_call | solution.py:314
  1.2 5.1 %collective-permute-start.4 = (bf16[3,8,2048]{2,1,0:T(8,128)(2,1)S(1)}, bf16[3,8,2048]{2,1,0:T(8,128)(2,1)S(1)}, u32[]{:S(2)}, u32[]{:S(2)}) collective-permute-start(bf16[3,8,2048]{2,1,0:T(8,128)(2,1)S(1)} %get-tuple-element.30), channel_id=1, source_target_pairs={{0,12},{4,8},{8,4},{12,0},{1,13},{5,9},{9,5},{13,1},{2,14},{6,10},... | collective-permute-start | bytes 294920 | tf_op jit(solution)/shard_map/ppermute | solution.py:286
  6.3 0.0 collective-permute-start.2
  6.3 0.6 %collective-permute-start = (bf16[3,8,2048]{2,1,0:T(8,128)(2,1)S(1)}, bf16[3,8,2048]{2,1,0:T(8,128)(2,1)S(1)}, u32[]{:S(2)}, u32[]{:S(2)}) collective-permute-start(bf16[3,8,2048]{2,1,0:T(8,128)(2,1)S(1)} %get-tuple-element.28), channel_id=1, source_target_pairs={{0,4},{4,0},{8,12},{12,8},{1,5},{5,1},{9,13},{13,9},{2,6},{6,2},{1... | collective-permute-start | bytes 294920 | tf_op jit(solution)/shard_map/ppermute | solution.py:286
  7.0 0.0 slice-start
  7.0 0.0 slice-start.1
  7.0 3.7 %suffix.1 = (f32[3,16,2048]{2,1,0:T(8,128)S(1)}, f32[3,16,2048]{2,1,0:T(8,128)S(1)}, bf16[2048,256]{1,0:T(8,128)(2,1)S(1)}, bf16[2048,256]{1,0:T(8,128)(2,1)S(1)}) custom-call(bf16[3,16,2048]{2,1,0:T(8,128)(2,1)S(1)} %get-tuple-element.25.q_ref, s32[16]{0:T(128)} %len_hbm.1, bf16[16,256,256]{2,1,0:T(8,128)(2,1)} %k_hbm.1, bf16[16,256,256]{2,1,0:T(8,128)(2,1)} %v_hbm.1, ...), custom_call_target="tpu_custom_call" | custom-call | flops 3000000000 | bytes 4194304 | tf_op jit(solution)/shard_map/suffix/pallas_call | solution.py:342
  10.7 0.0 collective-permute-done.4.q_ref
  10.7 1.5 %prompt.7 = bf16[3,8,2176]{2,1,0:T(8,128)(2,1)S(1)} custom-call(bf16[3,8,2048]{2,1,0:T(8,128)(2,1)S(1)} %collective-permute-done.4.q_ref, bf16[2048,256]{1,0:T(8,128)(2,1)S(1)} %get-tuple-element.26.k_ref, bf16[2048,256]{1,0:T(8,128)(2,1)S(1)} %get-tuple-element.27.v_ref), custom_call_target="tpu_custom_call" | custom-call | flops 402653184 | bytes 2097152 | tf_op jit(solution)/shard_map/prompt/pallas_call | solution.py:386
  12.2 3.8 %collective-permute-start.5 = (bf16[3,8,2176]{2,1,0:T(8,128)(2,1)S(1)}, bf16[3,8,2176]{2,1,0:T(8,128)(2,1)S(1)}, u32[]{:S(2)}, u32[]{:S(2)}) collective-permute-start(bf16[3,8,2176]{2,1,0:T(8,128)(2,1)S(1)} %prompt.7), channel_id=1, source_target_pairs={{0,12},{4,8},{8,4},{12,0},{1,13},{5,9},{9,5},{13,1},{2,14},{6,10},... | collective-permute-start | bytes 313352 | tf_op jit(solution)/shard_map/ppermute | solution.py:286
  16.0 0.0 collective-permute-done.2.q_ref
  16.0 1.5 %prompt.6 = bf16[3,8,2176]{2,1,0:T(8,128)(2,1)S(1)} custom-call(bf16[3,8,2048]{2,1,0:T(8,128)(2,1)S(1)} %collective-permute-done.2.q_ref, bf16[2048,256]{1,0:T(8,128)(2,1)S(1)} %get-tuple-element.26.k_ref, bf16[2048,256]{1,0:T(8,128)(2,1)S(1)} %get-tuple-element.27.v_ref), custom_call_target="tpu_custom_call" | custom-call | flops 402653184 | bytes 2097152 | tf_op jit(solution)/shard_map/prompt/pallas_call | solution.py:386
  17.5 1.1 %collective-permute-start.3 = (bf16[3,8,2176]{2,1,0:T(8,128)(2,1)S(1)}, bf16[3,8,2176]{2,1,0:T(8,128)(2,1)S(1)}, u32[]{:S(2)}, u32[]{:S(2)}) collective-permute-start(bf16[3,8,2176]{2,1,0:T(8,128)(2,1)S(1)} %prompt.6), channel_id=1, source_target_pairs={{0,8},{4,12},{8,0},{12,4},{1,9},{5,13},{9,1},{13,5},{2,10},{6,14},... | collective-permute-start | bytes 313352 | tf_op jit(solution)/shard_map/ppermute | solution.py:286
  18.6 0.0 collective-permute-done.q_ref
  18.6 1.5 %prompt.5 = bf16[3,8,2176]{2,1,0:T(8,128)(2,1)S(1)} custom-call(bf16[3,8,2048]{2,1,0:T(8,128)(2,1)S(1)} %collective-permute-done.q_ref, bf16[2048,256]{1,0:T(8,128)(2,1)S(1)} %get-tuple-element.26.k_ref, bf16[2048,256]{1,0:T(8,128)(2,1)S(1)} %get-tuple-element.27.v_ref), custom_call_target="tpu_custom_call" | custom-call | flops 402653184 | bytes 2097152 | tf_op jit(solution)/shard_map/prompt/pallas_call | solution.py:386
  20.1 0.7 %collective-permute-start.1 = (bf16[3,8,2176]{2,1,0:T(8,128)(2,1)S(1)}, bf16[3,8,2176]{2,1,0:T(8,128)(2,1)S(1)}, u32[]{:S(2)}, u32[]{:S(2)}) collective-permute-start(bf16[3,8,2176]{2,1,0:T(8,128)(2,1)S(1)} %prompt.5), channel_id=1, source_target_pairs={{0,4},{4,0},{8,12},{12,8},{1,5},{5,1},{9,13},{13,9},{2,6},{6,2},{1... | collective-permute-start | bytes 313352 | tf_op jit(solution)/shard_map/ppermute | solution.py:286
  20.8 1.5 %prompt.4.refs_1_ = bf16[3,8,2176]{2,1,0:T(8,128)(2,1)S(1)} custom-call(bf16[3,8,2048]{2,1,0:T(8,128)(2,1)S(1)} %get-tuple-element.24.q_ref, bf16[2048,256]{1,0:T(8,128)(2,1)S(1)} %get-tuple-element.26.k_ref, bf16[2048,256]{1,0:T(8,128)(2,1)S(1)} %get-tuple-element.27.v_ref), custom_call_target="tpu_custom_call" | custom-call | flops 402653184 | bytes 2097152 | tf_op jit(solution)/shard_map/prompt/pallas_call | solution.py:386
  22.4 0.0 collective-permute-done.5.refs_4_
  22.4 1.3 %collective-permute-done.3.refs_3_ = bf16[3,8,2176]{2,1,0:T(8,128)(2,1)S(1)} collective-permute-done((bf16[3,8,2176]{2,1,0:T(8,128)(2,1)S(1)}, bf16[3,8,2176]{2,1,0:T(8,128)(2,1)S(1)}, u32[]{:S(2)}, u32[]{:S(2)}) %collective-permute-start.3) | collective-permute-done | bytes 104480 | tf_op jit(solution)/shard_map/ppermute | solution.py:286
  23.7 1.2 %collective-permute-done.1.refs_2_ = bf16[3,8,2176]{2,1,0:T(8,128)(2,1)S(1)} collective-permute-done((bf16[3,8,2176]{2,1,0:T(8,128)(2,1)S(1)}, bf16[3,8,2176]{2,1,0:T(8,128)(2,1)S(1)}, u32[]{:S(2)}, u32[]{:S(2)}) %collective-permute-start.1) | collective-permute-done | bytes 104480 | tf_op jit(solution)/shard_map/ppermute | solution.py:286
  24.9 0.5 merge.1.refs_0_
  25.4 0.7 %collective-permute-start.9 = (bf16[3,16,2048]{2,1,0:T(8,128)(2,1)S(1)}, bf16[3,16,2048]{2,1,0:T(8,128)(2,1)S(1)}, u32[]{:S(2)}, u32[]{:S(2)}) collective-permute-start(bf16[3,16,2048]{2,1,0:T(8,128)(2,1)S(1)} %merge.1.refs_0_), channel_id=1, source_target_pairs={{4,8},{8,4},{5,9},{9,5},{6,10},{10,6},{7,11},{11,7},{20,24},{24,20... | collective-permute-start | bytes 589832 | tf_op jit(solution)/shard_map/ppermute | solution.py:412
  26.1 5.2 %collective-permute-start.8 = (bf16[3,16,2048]{2,1,0:T(8,128)(2,1)S(1)}, bf16[3,16,2048]{2,1,0:T(8,128)(2,1)S(1)}, u32[]{:S(2)}, u32[]{:S(2)}) collective-permute-start(bf16[3,16,2048]{2,1,0:T(8,128)(2,1)S(1)} %merge.1.refs_0_), channel_id=1, source_target_pairs={{0,8},{12,4},{1,9},{13,5},{2,10},{14,6},{3,11},{15,7},{16,24},{28,... | collective-permute-start | bytes 589832 | tf_op jit(solution)/shard_map/ppermute | solution.py:412
  31.3 0.1 collective-permute-start.6
  31.4 0.0 collective-permute-done.9.refs_2_
  31.4 1.3 %collective-permute-start.10 = (bf16[3,16,2048]{2,1,0:T(8,128)(2,1)S(1)}, bf16[3,16,2048]{2,1,0:T(8,128)(2,1)S(1)}, u32[]{:S(2)}, u32[]{:S(2)}) collective-permute-start(bf16[3,16,2048]{2,1,0:T(8,128)(2,1)S(1)} %collective-permute-done.9.refs_2_), channel_id=1, source_target_pairs={{8,12},{4,0},{9,13},{5,1},{10,14},{6,2},{11,15},{7,3},{24,28},{20,... | collective-permute-start | bytes 589832 | tf_op jit(solution)/shard_map/ppermute | solution.py:412
  32.7 3.4 %collective-permute-done.8.refs_0_ = bf16[3,16,2048]{2,1,0:T(8,128)(2,1)S(1)} collective-permute-done((bf16[3,16,2048]{2,1,0:T(8,128)(2,1)S(1)}, bf16[3,16,2048]{2,1,0:T(8,128)(2,1)S(1)}, u32[]{:S(2)}, u32[]{:S(2)}) %collective-permute-start.8) | collective-permute-done | bytes 196640 | tf_op jit(solution)/shard_map/ppermute | solution.py:412
  36.1 1.3 %collective-permute-start.11 = (bf16[3,16,2048]{2,1,0:T(8,128)(2,1)S(1)}, bf16[3,16,2048]{2,1,0:T(8,128)(2,1)S(1)}, u32[]{:S(2)}, u32[]{:S(2)}) collective-permute-start(bf16[3,16,2048]{2,1,0:T(8,128)(2,1)S(1)} %collective-permute-done.8.refs_0_), channel_id=1, source_target_pairs={{8,12},{4,0},{9,13},{5,1},{10,14},{6,2},{11,15},{7,3},{24,28},{20,... | collective-permute-start | bytes 589832 | tf_op jit(solution)/shard_map/ppermute | solution.py:412
  37.4 1.8 %collective-permute-done.6.refs_1_ = bf16[3,16,2048]{2,1,0:T(8,128)(2,1)S(1)} collective-permute-done((bf16[3,16,2048]{2,1,0:T(8,128)(2,1)S(1)}, bf16[3,16,2048]{2,1,0:T(8,128)(2,1)S(1)}, u32[]{:S(2)}, u32[]{:S(2)}) %collective-permute-start.6) | collective-permute-done | bytes 196640 | tf_op jit(solution)/shard_map/ppermute | solution.py:286
  39.2 0.0 slice-done
  39.2 0.0 slice-done.1
  39.2 2.7 %project.2 = (f32[3,16,2048]{2,1,0:T(8,128)S(1)}, bf16[3,16,2048]{2,1,0:T(8,128)(2,1)S(1)}) custom-call(bf16[3,16,2048]{2,1,0:T(8,128)(2,1)S(1)} %merge.1.refs_0_, bf16[3,16,2048]{2,1,0:T(8,128)(2,1)S(1)} %collective-permute-done.6.refs_1_, bf16[2048,2048]{1,0:T(8,128)(2,1)S(1)} %bitcast.9), custom_call_target="tpu_custom_call" | custom-call | flops 805306368 | bytes 8388608 | tf_op jit(solution)/shard_map/project/pallas_call | solution.py:428
  41.8 0.1 collective-permute-start.7
  41.9 0.6 %collective-permute-done.10.refs_1_ = bf16[3,16,2048]{2,1,0:T(8,128)(2,1)S(1)} collective-permute-done((bf16[3,16,2048]{2,1,0:T(8,128)(2,1)S(1)}, bf16[3,16,2048]{2,1,0:T(8,128)(2,1)S(1)}, u32[]{:S(2)}, u32[]{:S(2)}) %collective-permute-start.10) | collective-permute-done | bytes 196640 | tf_op jit(solution)/shard_map/ppermute | solution.py:412
  42.6 2.1 %collective-permute-done.11.refs_3_ = bf16[3,16,2048]{2,1,0:T(8,128)(2,1)S(1)} collective-permute-done((bf16[3,16,2048]{2,1,0:T(8,128)(2,1)S(1)}, bf16[3,16,2048]{2,1,0:T(8,128)(2,1)S(1)}, u32[]{:S(2)}, u32[]{:S(2)}) %collective-permute-start.11) | collective-permute-done | bytes 196640 | tf_op jit(solution)/shard_map/ppermute | solution.py:412
  44.7 2.7 %project.3 = (f32[3,16,2048]{2,1,0:T(8,128)S(1)}, bf16[3,16,2048]{2,1,0:T(8,128)(2,1)S(1)}) custom-call(bf16[3,16,2048]{2,1,0:T(8,128)(2,1)S(1)} %collective-permute-done.8.refs_0_, bf16[3,16,2048]{2,1,0:T(8,128)(2,1)S(1)} %collective-permute-done.10.refs_1_, bf16[3,16,2048]{2,1,0:T(8,128)(2,1)S(1)} %collective-permute-done.9.refs_2_, ...), custom_call_target="tpu_custom_call" | custom-call | flops 805306368 | bytes 8388608 | tf_op jit(solution)/shard_map/project/pallas_call | solution.py:428
  47.4 0.1 collective-permute-start.12
  47.4 0.0 collective-permute-done.7.got_ref
  47.5 1.3 %collective-permute-start.13 = (bf16[3,16,2048]{2,1,0:T(8,128)(2,1)S(1)}, bf16[3,16,2048]{2,1,0:T(8,128)(2,1)S(1)}, u32[]{:S(2)}, u32[]{:S(2)}) collective-permute-start(bf16[3,16,2048]{2,1,0:T(8,128)(2,1)S(1)} %get-tuple-element.39), channel_id=1, source_target_pairs={{2,0},{3,1},{6,4},{7,5},{8,10},{9,11},{12,14},{13,15},{18,16},{19,... | collective-permute-start | bytes 589832 | tf_op jit(solution)/shard_map/ppermute | solution.py:421
  48.8 0.1 collective-permute-done.12.got_ref
  48.9 4.5 %collective-permute-start.14 = (bf16[3,16,2048]{2,1,0:T(8,128)(2,1)S(1)}, bf16[3,16,2048]{2,1,0:T(8,128)(2,1)S(1)}, u32[]{:S(2)}, u32[]{:S(2)}) collective-permute-start(bf16[3,16,2048]{2,1,0:T(8,128)(2,1)S(1)} %get-tuple-element.40), channel_id=1, source_target_pairs={{0,2},{1,3},{4,6},{5,7},{10,8},{11,9},{14,12},{15,13},{16,18},{17,... | collective-permute-start | bytes 589832 | tf_op jit(solution)/shard_map/ppermute | solution.py:421
  53.4 3.2 %collective-permute-done.13 = bf16[3,16,2048]{2,1,0:T(8,128)(2,1)S(1)} collective-permute-done((bf16[3,16,2048]{2,1,0:T(8,128)(2,1)S(1)}, bf16[3,16,2048]{2,1,0:T(8,128)(2,1)S(1)}, u32[]{:S(2)}, u32[]{:S(2)}) %collective-permute-start.13) | collective-permute-done | bytes 196640 | tf_op jit(solution)/shard_map/ppermute | solution.py:421
  56.7 1.3 %collective-permute-done.14 = bf16[3,16,2048]{2,1,0:T(8,128)(2,1)S(1)} collective-permute-done((bf16[3,16,2048]{2,1,0:T(8,128)(2,1)S(1)}, bf16[3,16,2048]{2,1,0:T(8,128)(2,1)S(1)}, u32[]{:S(2)}, u32[]{:S(2)}) %collective-permute-start.14) | collective-permute-done | bytes 196640 | tf_op jit(solution)/shard_map/ppermute | solution.py:421
  57.9 0.8 %fusion = bf16[16,3,2048]{2,0,1:T(8,128)(2,1)} fusion(bf16[3,16,2048]{2,1,0:T(8,128)(2,1)S(1)} %collective-permute-done.14, bf16[3,16,2048]{2,1,0:T(8,128)(2,1)S(1)} %collective-permute-done.13, f32[3,16,2048]{2,1,0:T(8,128)S(1)} %get-tuple-element.35, f32[3,16,2048]{2,1,0:T(8,128)S(1)} %get-tuple-element.38, pred[]{:T(512)S(6)} %eq.3), kind=kLoop, calls=%fused_computation.1 | loop fusion | flops 589824 | bytes 1376257 | tf_op jit(solution)/shard_map/transpose | solution.py:470
  (3 shorter events, 0.1 us)
Async XLA Ops:
  1.2 9.5 %collective-permute-start.4 = (bf16[3,8,2048]{2,1,0:T(8,128)(2,1)S(1)}, bf16[3,8,2048]{2,1,0:T(8,128)(2,1)S(1)}, u32[]{:S(2)}, u32[]{:S(2)}) collective-permute-start(bf16[3,8,2048]{2,1,0:T(8,128)(2,1)S(1)} %get-tuple-element.30), channel_id=1, source_target_pairs={{0,12},{4,8},{8,4},{12,0},{1,13},{5,9},{9,5},{13,1},{2,14},{6,10},... | collective-permute-start | bytes 294920 | tf_op jit(solution)/shard_map/ppermute | solution.py:286
  6.3 9.7 %collective-permute-start.2 = (bf16[3,8,2048]{2,1,0:T(8,128)(2,1)S(1)}, bf16[3,8,2048]{2,1,0:T(8,128)(2,1)S(1)}, u32[]{:S(2)}, u32[]{:S(2)}) collective-permute-start(bf16[3,8,2048]{2,1,0:T(8,128)(2,1)S(1)} %get-tuple-element.29), channel_id=1, source_target_pairs={{0,8},{4,12},{8,0},{12,4},{1,9},{5,13},{9,1},{13,5},{2,10},{6,14},... | collective-permute-start | bytes 294920 | tf_op jit(solution)/shard_map/ppermute | solution.py:286
  6.3 12.3 %collective-permute-start = (bf16[3,8,2048]{2,1,0:T(8,128)(2,1)S(1)}, bf16[3,8,2048]{2,1,0:T(8,128)(2,1)S(1)}, u32[]{:S(2)}, u32[]{:S(2)}) collective-permute-start(bf16[3,8,2048]{2,1,0:T(8,128)(2,1)S(1)} %get-tuple-element.28), channel_id=1, source_target_pairs={{0,4},{4,0},{8,12},{12,8},{1,5},{5,1},{9,13},{13,9},{2,6},{6,2},{1... | collective-permute-start | bytes 294920 | tf_op jit(solution)/shard_map/ppermute | solution.py:286
  7.0 32.2 %slice-start = ((s8[8388608]{0:T(1024)(128)(4,1)}), s8[4194304]{0:T(1024)(128)(4,1)S(1)}, s32[]{:S(2)}) async-start(s8[8388608]{0:T(1024)(128)(4,1)} %bitcast.8), calls=%async_computation | async-start | bytes 8388608
  7.0 32.2 %slice-start.1 = ((s8[8388608]{0:T(1024)(128)(4,1)}), s8[4194304]{0:T(1024)(128)(4,1)S(1)}, s32[]{:S(2)}) async-start(s8[8388608]{0:T(1024)(128)(4,1)} %bitcast.8), calls=%async_computation.1 | async-start | bytes 8388608
  12.2 10.2 %collective-permute-start.5 = (bf16[3,8,2176]{2,1,0:T(8,128)(2,1)S(1)}, bf16[3,8,2176]{2,1,0:T(8,128)(2,1)S(1)}, u32[]{:S(2)}, u32[]{:S(2)}) collective-permute-start(bf16[3,8,2176]{2,1,0:T(8,128)(2,1)S(1)} %prompt.7), channel_id=1, source_target_pairs={{0,12},{4,8},{8,4},{12,0},{1,13},{5,9},{9,5},{13,1},{2,14},{6,10},... | collective-permute-start | bytes 313352 | tf_op jit(solution)/shard_map/ppermute | solution.py:286
  17.5 6.1 %collective-permute-start.3 = (bf16[3,8,2176]{2,1,0:T(8,128)(2,1)S(1)}, bf16[3,8,2176]{2,1,0:T(8,128)(2,1)S(1)}, u32[]{:S(2)}, u32[]{:S(2)}) collective-permute-start(bf16[3,8,2176]{2,1,0:T(8,128)(2,1)S(1)} %prompt.6), channel_id=1, source_target_pairs={{0,8},{4,12},{8,0},{12,4},{1,9},{5,13},{9,1},{13,5},{2,10},{6,14},... | collective-permute-start | bytes 313352 | tf_op jit(solution)/shard_map/ppermute | solution.py:286
  20.1 4.7 %collective-permute-start.1 = (bf16[3,8,2176]{2,1,0:T(8,128)(2,1)S(1)}, bf16[3,8,2176]{2,1,0:T(8,128)(2,1)S(1)}, u32[]{:S(2)}, u32[]{:S(2)}) collective-permute-start(bf16[3,8,2176]{2,1,0:T(8,128)(2,1)S(1)} %prompt.5), channel_id=1, source_target_pairs={{0,4},{4,0},{8,12},{12,8},{1,5},{5,1},{9,13},{13,9},{2,6},{6,2},{1... | collective-permute-start | bytes 313352 | tf_op jit(solution)/shard_map/ppermute | solution.py:286
  25.4 6.0 %collective-permute-start.9 = (bf16[3,16,2048]{2,1,0:T(8,128)(2,1)S(1)}, bf16[3,16,2048]{2,1,0:T(8,128)(2,1)S(1)}, u32[]{:S(2)}, u32[]{:S(2)}) collective-permute-start(bf16[3,16,2048]{2,1,0:T(8,128)(2,1)S(1)} %merge.1.refs_0_), channel_id=1, source_target_pairs={{4,8},{8,4},{5,9},{9,5},{6,10},{10,6},{7,11},{11,7},{20,24},{24,20... | collective-permute-start | bytes 589832 | tf_op jit(solution)/shard_map/ppermute | solution.py:412
  26.1 10.0 %collective-permute-start.8 = (bf16[3,16,2048]{2,1,0:T(8,128)(2,1)S(1)}, bf16[3,16,2048]{2,1,0:T(8,128)(2,1)S(1)}, u32[]{:S(2)}, u32[]{:S(2)}) collective-permute-start(bf16[3,16,2048]{2,1,0:T(8,128)(2,1)S(1)} %merge.1.refs_0_), channel_id=1, source_target_pairs={{0,8},{12,4},{1,9},{13,5},{2,10},{14,6},{3,11},{15,7},{16,24},{28,... | collective-permute-start | bytes 589832 | tf_op jit(solution)/shard_map/ppermute | solution.py:412
  31.3 7.8 %collective-permute-start.6 = (bf16[3,16,2048]{2,1,0:T(8,128)(2,1)S(1)}, bf16[3,16,2048]{2,1,0:T(8,128)(2,1)S(1)}, u32[]{:S(2)}, u32[]{:S(2)}) collective-permute-start(bf16[3,16,2048]{2,1,0:T(8,128)(2,1)S(1)} %merge.1.refs_0_), channel_id=1, source_target_pairs={{0,4},{4,0},{8,12},{12,8},{1,5},{5,1},{9,13},{13,9},{2,6},{6,2},{1... | collective-permute-start | bytes 589832 | tf_op jit(solution)/shard_map/ppermute | solution.py:286
  31.4 11.2 %collective-permute-start.10 = (bf16[3,16,2048]{2,1,0:T(8,128)(2,1)S(1)}, bf16[3,16,2048]{2,1,0:T(8,128)(2,1)S(1)}, u32[]{:S(2)}, u32[]{:S(2)}) collective-permute-start(bf16[3,16,2048]{2,1,0:T(8,128)(2,1)S(1)} %collective-permute-done.9.refs_2_), channel_id=1, source_target_pairs={{8,12},{4,0},{9,13},{5,1},{10,14},{6,2},{11,15},{7,3},{24,28},{20,... | collective-permute-start | bytes 589832 | tf_op jit(solution)/shard_map/ppermute | solution.py:412
  36.1 8.6 %collective-permute-start.11 = (bf16[3,16,2048]{2,1,0:T(8,128)(2,1)S(1)}, bf16[3,16,2048]{2,1,0:T(8,128)(2,1)S(1)}, u32[]{:S(2)}, u32[]{:S(2)}) collective-permute-start(bf16[3,16,2048]{2,1,0:T(8,128)(2,1)S(1)} %collective-permute-done.8.refs_0_), channel_id=1, source_target_pairs={{8,12},{4,0},{9,13},{5,1},{10,14},{6,2},{11,15},{7,3},{24,28},{20,... | collective-permute-start | bytes 589832 | tf_op jit(solution)/shard_map/ppermute | solution.py:412
  41.8 5.6 %collective-permute-start.7 = (bf16[3,16,2048]{2,1,0:T(8,128)(2,1)S(1)}, bf16[3,16,2048]{2,1,0:T(8,128)(2,1)S(1)}, u32[]{:S(2)}, u32[]{:S(2)}) collective-permute-start(bf16[3,16,2048]{2,1,0:T(8,128)(2,1)S(1)} %get-tuple-element.34), channel_id=1, source_target_pairs={{0,1},{1,0},{2,3},{3,2},{4,5},{5,4},{6,7},{7,6},{8,9},{9,8},{10,11... | collective-permute-start | bytes 589832 | tf_op jit(solution)/shard_map/ppermute | solution.py:286
  47.4 1.5 %collective-permute-start.12 = (bf16[3,16,2048]{2,1,0:T(8,128)(2,1)S(1)}, bf16[3,16,2048]{2,1,0:T(8,128)(2,1)S(1)}, u32[]{:S(2)}, u32[]{:S(2)}) collective-permute-start(bf16[3,16,2048]{2,1,0:T(8,128)(2,1)S(1)} %get-tuple-element.37), channel_id=1, source_target_pairs={{0,1},{1,0},{2,3},{3,2},{4,5},{5,4},{6,7},{7,6},{8,9},{9,8},{10,11... | collective-permute-start | bytes 589832 | tf_op jit(solution)/shard_map/ppermute | solution.py:286
  47.5 9.2 %collective-permute-start.13 = (bf16[3,16,2048]{2,1,0:T(8,128)(2,1)S(1)}, bf16[3,16,2048]{2,1,0:T(8,128)(2,1)S(1)}, u32[]{:S(2)}, u32[]{:S(2)}) collective-permute-start(bf16[3,16,2048]{2,1,0:T(8,128)(2,1)S(1)} %get-tuple-element.39), channel_id=1, source_target_pairs={{2,0},{3,1},{6,4},{7,5},{8,10},{9,11},{12,14},{13,15},{18,16},{19,... | collective-permute-start | bytes 589832 | tf_op jit(solution)/shard_map/ppermute | solution.py:421
  48.9 9.0 %collective-permute-start.14 = (bf16[3,16,2048]{2,1,0:T(8,128)(2,1)S(1)}, bf16[3,16,2048]{2,1,0:T(8,128)(2,1)S(1)}, u32[]{:S(2)}, u32[]{:S(2)}) collective-permute-start(bf16[3,16,2048]{2,1,0:T(8,128)(2,1)S(1)} %get-tuple-element.40), channel_id=1, source_target_pairs={{0,2},{1,3},{4,6},{5,7},{10,8},{11,9},{14,12},{15,13},{16,18},{17,... | collective-permute-start | bytes 589832 | tf_op jit(solution)/shard_map/ppermute | solution.py:421

commit v4 on v2

--- a/solution.py
+++ b/solution.py
@@ -7,6 +7,7 @@
 from jax.experimental import pallas as pl
 from jax.experimental.pallas import tpu as pltpu
 from jax.sharding import PartitionSpec as P
+
 
 HD = 128
 LANES = 128
@@ -237,36 +238,34 @@
             out_ref[s, :, lanes] = mixed.astype(BF16)
 
 
-def project_kernel(owners, parts, *refs):
-    rows_refs, w_ref, own_ref, send_refs, held = (
-        refs[:owners],
-        refs[owners],
-        refs[owners + 1],
-        refs[owners + 2 : -1],
-        refs[-1],
-    )
-    steps, count, _ = rows_refs[0].shape
+def project_kernel(own_ref, g1_ref, g2_ref, g3_ref, w_ref, own_out, far_out, beside_out, held):
+    steps, count, _ = own_ref.shape
     each = steps * count
-
-    @pl.when(pl.program_id(0) == 0)
-    def _():
-        me, mine = lax.axis_index("dp"), lax.axis_index("kv")
-        for shift, ref in enumerate(rows_refs):
-            place = (me ^ shift) ^ mine
+    me, mine = lax.axis_index("dp"), lax.axis_index("kv")
+    for shift, ref in enumerate((own_ref, g1_ref, g2_ref, g3_ref)):
+        place = (me ^ shift) ^ mine
+        for s in range(steps):
+            held[place, pl.ds(s * count, count), :] = ref[s]
+    rows = held[...].reshape(4 * each, held.shape[2])
+    outs = (own_out, beside_out.at[0], far_out, beside_out.at[1])
+    chunk = 512
+    for at in range(0, w_ref.shape[1], chunk):
+        lanes = pl.ds(at, chunk)
+        product = jnp.dot(rows, w_ref[:, lanes], preferred_element_type=F32)
+        for part, ref in enumerate(outs):
             for s in range(steps):
-                held[place, pl.ds(s * count, count), :] = ref[s]
-
-    product = jnp.dot(
-        held[...].reshape(parts * each, held.shape[2]), w_ref[...], preferred_element_type=F32
-    )
-    for part, ref in enumerate((own_ref, *send_refs)):
-        for s in range(steps):
-            at = part * each + s * count
-            ref[s] = product[at : at + count].astype(ref.dtype)
+                row = part * each + s * count
+                ref[s, :, lanes] = product[row : row + count].astype(ref.dtype)
+
+
+def add_kernel(keep_ref, got_ref, send_ref):
+    for s in range(keep_ref.shape[0]):
+        send_ref[s] = (keep_ref[s] + got_ref[1, s].astype(F32)).astype(BF16)
 
 
 def swap(values, axis, mask):
-    return lax.ppermute(values, axis, [(i, i ^ mask) for i in range(lax.axis_size(axis))])
+    pairs = [(i, i ^ mask) for i in range(lax.axis_size(axis))]
+    return lax.ppermute(values, axis, pairs)
 
 
 def local(
@@ -315,7 +314,7 @@
         return moved.reshape(steps, owners * capacity, -1)
 
     if direct:
-        received = [packed[0]] + [swap(packed[mask], "dp", mask) for mask in (1, 2, 3)]
+        received = [packed[0]] + [swap(packed[i], "dp", i) for i in (1, 2, 3)]
     else:
         received = [all_to_all(packed[0])]
 
@@ -364,9 +363,11 @@
         cost_estimate=cost(4 * size * steps * width * prefix_keys.shape[1], prefix_keys.size * 4),
         name="prompt",
     )
-    answers = [prompt(block, keys, values) for block in received]
+    answers = []
+    for asked in received:
+        answers.append(prompt(asked, keys, values))
     if direct:
-        home = [answers[0]] + [swap(answers[mask], "dp", mask) for mask in (1, 2, 3)]
+        home = [answers[0]] + [swap(answers[i], "dp", i) for i in (1, 2, 3)]
     else:
         home = [all_to_all(answers[0])]
 
@@ -389,24 +390,36 @@
         total = lax.psum_scatter(product, "kv", scatter_dimension=1, tiled=True)
         return total.astype(BF16).transpose(1, 0, 2)
 
-    gathered = [attended] + [swap(attended, "dp", mask) for mask in (1, 2, 3)]
-    chunk = columns // 4
-    own_sum, *sent = pl.pallas_call(
-        functools.partial(project_kernel, owners, parts),
-        grid=(columns // chunk,),
-        out_shape=[jax.ShapeDtypeStruct((steps, count, columns), F32)]
-        + [jax.ShapeDtypeStruct((steps, count, columns), BF16)] * (parts - 1),
-        in_specs=[pl.BlockSpec((steps, count, width), lambda i: (0, 0, 0))] * owners
-        + [pl.BlockSpec((width, chunk), lambda i: (0, i))],
-        out_specs=[pl.BlockSpec((steps, count, chunk), lambda i: (0, 0, i))] * parts,
-        scratch_shapes=[pltpu.VMEM((parts, steps * count, width), BF16)],
-        compiler_params=params(24),
+    by_two = swap(attended, "dp", 2)
+    by_one = swap(attended, "dp", 1)
+    by_three = swap(attended, "dp", 3)
+    piece = (steps, count, columns)
+    own_sum, far_sum, beside = pl.pallas_call(
+        project_kernel,
+        out_shape=[
+            jax.ShapeDtypeStruct(piece, F32),
+            jax.ShapeDtypeStruct(piece, F32),
+            jax.ShapeDtypeStruct((2, *piece), BF16),
+        ],
+        in_specs=[vmem] * 5,
+        out_specs=[vmem] * 3,
+        scratch_shapes=[pltpu.VMEM((owners, steps * count, width), BF16)],
+        compiler_params=params(8),
         cost_estimate=cost(2 * owners * steps * count * width * columns, out_weight.size * 2),
         name="project",
-    )(*gathered, out_weight)
-    total = own_sum
-    for shift, values in enumerate(sent, 1):
-        total = total + swap(values, "kv", shift).astype(F32)
+    )(attended, by_one, by_two, by_three, out_weight)
+    got = swap(beside, "kv", 1)
+    sent = pl.pallas_call(
+        add_kernel,
+        out_shape=jax.ShapeDtypeStruct(piece, BF16),
+        in_specs=[vmem] * 2,
+        out_specs=vmem,
+        compiler_params=params(4),
+        cost_estimate=cost(far_sum.size, far_sum.size * 12),
+        name="add",
+    )(far_sum, got)
+    came = swap(sent, "kv", 2)
+    total = own_sum + got[0].astype(F32) + came.astype(F32)
     return total.astype(BF16).transpose(1, 0, 2)
 
 

time: 59.9 us -> 56.3 us (0.940)
  waiting for transfers between devices: 28.7 us -> 26.7 us
  Pallas kernels: 14.6 us -> 13.3 us
    ppermute x12 -> x11, waiting for transfers between devices: 28.7 us -> 26.7 us  [swap(): return lax.ppermute(values, axis, pairs)]
    pallas_call x5 -> x6, Pallas kernels: 9.25 us -> 7.94 us  [the longest x4 6.06 us: local(): answers.append(prompt(asked, keys, values))]
    ppermute x12 -> x11, starting transfers between devices: 15.6 us -> 15.3 us  [swap(): return lax.ppermute(values, axis, pairs)]
  transfers between devices with their start and end apart: 12 -> 11, of which waited for: 7 -> 7; matrix products, arithmetic and copies ran while one was open for 0% -> 0% of each run, Pallas kernels for 16% -> 17%
where the time goes in v4:
time: 56.3 us; the launch traced here: 56.2 us
  waiting for transfers between devices  26.7 us (47%)
  starting transfers between devices  15.3 us (27%)
  Pallas kernels  13.3 us (24%)
  other arithmetic  0.75 us (1%)
    ppermute x11, waiting for transfers between devices, swap(): return lax.ppermute(values, axis, pairs)  26.7 us
    ppermute x11, starting transfers between devices, swap(): return lax.ppermute(values, axis, pairs)  15.3 us
    pallas_call x4, Pallas kernels, local(): answers.append(prompt(asked, keys, values))  6.06 us
    pallas_call x1, Pallas kernels, local(): pl.pallas_call(functools.partial(suffix_kernel, group), out_shape=[jax.Sh...  3.7 us
    pallas_call x1, Pallas kernels, local(): pl.pallas_call(project_kernel, out_shape=[jax.ShapeDtypeStruct(piece, F32...  1.83 us
    pallas_call x1, Pallas kernels, local(): pl.pallas_call(functools.partial(pack_kernel, capacity, direct), out_shap...  1.17 us
  transfers between devices with their start and end apart: 11, of which 7 were waited for; matrix products, arithmetic and copies ran while one was open for 0% of the time, Pallas kernels for 17%

profile of v4, /device:TPU:0, one launch (start us, length us, event | category | flops | bytes accessed | tf_op | source)
XLA Modules:
  0.0 56.2 jit_solution(16848502244181112502)
XLA Ops:
  0.0 1.2 %pack.1 = (bf16[3,16,2048]{2,1,0:T(8,128)(2,1)S(1)}, bf16[16,32]{1,0:T(8,128)(2,1)S(1)}, bf16[3,8,2048]{2,1,0:T(8,128)(2,1)S(1)}, bf16[3,8,2048]{2,1,0:T(8,128)(...) custom-call(s32[16]{0:T(128)} %bitcast.16, bf16[3,16,2048]{2,1,0:T(8,128)(2,1)} %bitcast.15), custom_call_target="tpu_custom_call" | custom-call | flops 6291456 | bytes 1048576 | tf_op jit(solution)/shard_map/pack/pallas_call | solution.py:296
  1.2 3.1 %collective-permute-start = (bf16[3,8,2048]{2,1,0:T(8,128)(2,1)S(1)}, bf16[3,8,2048]{2,1,0:T(8,128)(2,1)S(1)}, u32[]{:S(2)}, u32[]{:S(2)}) collective-permute-start(bf16[3,8,2048]{2,1,0:T(8,128)(2,1)S(1)} %get-tuple-element.23), channel_id=1, source_target_pairs={{0,4},{4,0},{8,12},{12,8},{1,5},{5,1},{9,13},{13,9},{2,6},{6,2},{1... | collective-permute-start | bytes 294920 | tf_op jit(solution)/shard_map/ppermute | solution.py:268
  4.3 2.6 %collective-permute-start.2 = (bf16[3,8,2048]{2,1,0:T(8,128)(2,1)S(1)}, bf16[3,8,2048]{2,1,0:T(8,128)(2,1)S(1)}, u32[]{:S(2)}, u32[]{:S(2)}) collective-permute-start(bf16[3,8,2048]{2,1,0:T(8,128)(2,1)S(1)} %get-tuple-element.24), channel_id=1, source_target_pairs={{0,8},{4,12},{8,0},{12,4},{1,9},{5,13},{9,1},{13,5},{2,10},{6,14},... | collective-permute-start | bytes 294920 | tf_op jit(solution)/shard_map/ppermute | solution.py:268
  6.9 0.0 collective-permute-start.4
  6.9 0.0 slice-start
  6.9 0.0 slice-start.1
  6.9 3.7 %suffix.1 = (f32[3,16,2048]{2,1,0:T(8,128)S(1)}, f32[3,16,2048]{2,1,0:T(8,128)S(1)}, bf16[2048,256]{1,0:T(8,128)(2,1)S(1)}, bf16[2048,256]{1,0:T(8,128)(2,1)S(1)}) custom-call(bf16[3,16,2048]{2,1,0:T(8,128)(2,1)S(1)} %get-tuple-element.20.q_ref, s32[16]{0:T(128)} %len_hbm.1, bf16[16,256,256]{2,1,0:T(8,128)(2,1)} %k_hbm.1, bf16[16,256,256]{2,1,0:T(8,128)(2,1)} %v_hbm.1, ...), custom_call_target="tpu_custom_call" | custom-call | flops 3000000000 | bytes 4194304 | tf_op jit(solution)/shard_map/suffix/pallas_call | solution.py:324
  10.6 0.0 collective-permute-done.q_ref
  10.6 1.5 %prompt.5 = bf16[3,8,2176]{2,1,0:T(8,128)(2,1)S(1)} custom-call(bf16[3,8,2048]{2,1,0:T(8,128)(2,1)S(1)} %collective-permute-done.q_ref, bf16[2048,256]{1,0:T(8,128)(2,1)S(1)} %get-tuple-element.21.k_ref, bf16[2048,256]{1,0:T(8,128)(2,1)S(1)} %get-tuple-element.22.v_ref), custom_call_target="tpu_custom_call" | custom-call | flops 402653184 | bytes 2097152 | tf_op jit(solution)/shard_map/prompt/pallas_call | solution.py:368
  12.1 1.0 %collective-permute-start.1 = (bf16[3,8,2176]{2,1,0:T(8,128)(2,1)S(1)}, bf16[3,8,2176]{2,1,0:T(8,128)(2,1)S(1)}, u32[]{:S(2)}, u32[]{:S(2)}) collective-permute-start(bf16[3,8,2176]{2,1,0:T(8,128)(2,1)S(1)} %prompt.5), channel_id=1, source_target_pairs={{0,4},{4,0},{8,12},{12,8},{1,5},{5,1},{9,13},{13,9},{2,6},{6,2},{1... | collective-permute-start | bytes 313352 | tf_op jit(solution)/shard_map/ppermute | solution.py:268
  13.1 1.7 %collective-permute-done.2.q_ref = bf16[3,8,2048]{2,1,0:T(8,128)(2,1)S(1)} collective-permute-done((bf16[3,8,2048]{2,1,0:T(8,128)(2,1)S(1)}, bf16[3,8,2048]{2,1,0:T(8,128)(2,1)S(1)}, u32[]{:S(2)}, u32[]{:S(2)}) %collective-permute-start.2) | collective-permute-done | bytes 98336 | tf_op jit(solution)/shard_map/ppermute | solution.py:268
  14.8 1.5 %prompt.6 = bf16[3,8,2176]{2,1,0:T(8,128)(2,1)S(1)} custom-call(bf16[3,8,2048]{2,1,0:T(8,128)(2,1)S(1)} %collective-permute-done.2.q_ref, bf16[2048,256]{1,0:T(8,128)(2,1)S(1)} %get-tuple-element.21.k_ref, bf16[2048,256]{1,0:T(8,128)(2,1)S(1)} %get-tuple-element.22.v_ref), custom_call_target="tpu_custom_call" | custom-call | flops 402653184 | bytes 2097152 | tf_op jit(solution)/shard_map/prompt/pallas_call | solution.py:368
  16.3 1.8 %collective-permute-start.3 = (bf16[3,8,2176]{2,1,0:T(8,128)(2,1)S(1)}, bf16[3,8,2176]{2,1,0:T(8,128)(2,1)S(1)}, u32[]{:S(2)}, u32[]{:S(2)}) collective-permute-start(bf16[3,8,2176]{2,1,0:T(8,128)(2,1)S(1)} %prompt.6), channel_id=1, source_target_pairs={{0,8},{4,12},{8,0},{12,4},{1,9},{5,13},{9,1},{13,5},{2,10},{6,14},... | collective-permute-start | bytes 313352 | tf_op jit(solution)/shard_map/ppermute | solution.py:268
  18.2 0.0 collective-permute-done.4.q_ref
  18.2 1.5 %prompt.7 = bf16[3,8,2176]{2,1,0:T(8,128)(2,1)S(1)} custom-call(bf16[3,8,2048]{2,1,0:T(8,128)(2,1)S(1)} %collective-permute-done.4.q_ref, bf16[2048,256]{1,0:T(8,128)(2,1)S(1)} %get-tuple-element.21.k_ref, bf16[2048,256]{1,0:T(8,128)(2,1)S(1)} %get-tuple-element.22.v_ref), custom_call_target="tpu_custom_call" | custom-call | flops 402653184 | bytes 2097152 | tf_op jit(solution)/shard_map/prompt/pallas_call | solution.py:368
  19.7 0.7 %collective-permute-start.5 = (bf16[3,8,2176]{2,1,0:T(8,128)(2,1)S(1)}, bf16[3,8,2176]{2,1,0:T(8,128)(2,1)S(1)}, u32[]{:S(2)}, u32[]{:S(2)}) collective-permute-start(bf16[3,8,2176]{2,1,0:T(8,128)(2,1)S(1)} %prompt.7), channel_id=1, source_target_pairs={{0,12},{4,8},{8,4},{12,0},{1,13},{5,9},{9,5},{13,1},{2,14},{6,10},... | collective-permute-start | bytes 313352 | tf_op jit(solution)/shard_map/ppermute | solution.py:268
  20.4 1.5 %prompt.4.refs_1_ = bf16[3,8,2176]{2,1,0:T(8,128)(2,1)S(1)} custom-call(bf16[3,8,2048]{2,1,0:T(8,128)(2,1)S(1)} %get-tuple-element.19.q_ref, bf16[2048,256]{1,0:T(8,128)(2,1)S(1)} %get-tuple-element.21.k_ref, bf16[2048,256]{1,0:T(8,128)(2,1)S(1)} %get-tuple-element.22.v_ref), custom_call_target="tpu_custom_call" | custom-call | flops 402653184 | bytes 2097152 | tf_op jit(solution)/shard_map/prompt/pallas_call | solution.py:368
  21.9 0.0 collective-permute-done.1.refs_2_
  21.9 2.9 %collective-permute-done.3.refs_3_ = bf16[3,8,2176]{2,1,0:T(8,128)(2,1)S(1)} collective-permute-done((bf16[3,8,2176]{2,1,0:T(8,128)(2,1)S(1)}, bf16[3,8,2176]{2,1,0:T(8,128)(2,1)S(1)}, u32[]{:S(2)}, u32[]{:S(2)}) %collective-permute-start.3) | collective-permute-done | bytes 104480 | tf_op jit(solution)/shard_map/ppermute | solution.py:268
  24.8 1.5 %collective-permute-done.5.refs_4_ = bf16[3,8,2176]{2,1,0:T(8,128)(2,1)S(1)} collective-permute-done((bf16[3,8,2176]{2,1,0:T(8,128)(2,1)S(1)}, bf16[3,8,2176]{2,1,0:T(8,128)(2,1)S(1)}, u32[]{:S(2)}, u32[]{:S(2)}) %collective-permute-start.5) | collective-permute-done | bytes 104480 | tf_op jit(solution)/shard_map/ppermute | solution.py:268
  26.3 0.5 merge.1.own_ref
  26.8 1.7 %collective-permute-start.8 = (bf16[3,16,2048]{2,1,0:T(8,128)(2,1)S(1)}, bf16[3,16,2048]{2,1,0:T(8,128)(2,1)S(1)}, u32[]{:S(2)}, u32[]{:S(2)}) collective-permute-start(bf16[3,16,2048]{2,1,0:T(8,128)(2,1)S(1)} %merge.1.own_ref), channel_id=1, source_target_pairs={{0,12},{4,8},{8,4},{12,0},{1,13},{5,9},{9,5},{13,1},{2,14},{6,10},... | collective-permute-start | bytes 589832 | tf_op jit(solution)/shard_map/ppermute | solution.py:268
  28.6 1.1 %collective-permute-start.7 = (bf16[3,16,2048]{2,1,0:T(8,128)(2,1)S(1)}, bf16[3,16,2048]{2,1,0:T(8,128)(2,1)S(1)}, u32[]{:S(2)}, u32[]{:S(2)}) collective-permute-start(bf16[3,16,2048]{2,1,0:T(8,128)(2,1)S(1)} %merge.1.own_ref), channel_id=1, source_target_pairs={{0,8},{4,12},{8,0},{12,4},{1,9},{5,13},{9,1},{13,5},{2,10},{6,14},... | collective-permute-start | bytes 589832 | tf_op jit(solution)/shard_map/ppermute | solution.py:268
  29.6 1.7 %collective-permute-start.6 = (bf16[3,16,2048]{2,1,0:T(8,128)(2,1)S(1)}, bf16[3,16,2048]{2,1,0:T(8,128)(2,1)S(1)}, u32[]{:S(2)}, u32[]{:S(2)}) collective-permute-start(bf16[3,16,2048]{2,1,0:T(8,128)(2,1)S(1)} %merge.1.own_ref), channel_id=1, source_target_pairs={{0,4},{4,0},{8,12},{12,8},{1,5},{5,1},{9,13},{13,9},{2,6},{6,2},{1... | collective-permute-start | bytes 589832 | tf_op jit(solution)/shard_map/ppermute | solution.py:268
  31.3 5.2 %collective-permute-done.8.g3_ref = bf16[3,16,2048]{2,1,0:T(8,128)(2,1)S(1)} collective-permute-done((bf16[3,16,2048]{2,1,0:T(8,128)(2,1)S(1)}, bf16[3,16,2048]{2,1,0:T(8,128)(2,1)S(1)}, u32[]{:S(2)}, u32[]{:S(2)}) %collective-permute-start.8) | collective-permute-done | bytes 196640 | tf_op jit(solution)/shard_map/ppermute | solution.py:268
  36.5 8.2 %collective-permute-done.7.g2_ref = bf16[3,16,2048]{2,1,0:T(8,128)(2,1)S(1)} collective-permute-done((bf16[3,16,2048]{2,1,0:T(8,128)(2,1)S(1)}, bf16[3,16,2048]{2,1,0:T(8,128)(2,1)S(1)}, u32[]{:S(2)}, u32[]{:S(2)}) %collective-permute-start.7) | collective-permute-done | bytes 196640 | tf_op jit(solution)/shard_map/ppermute | solution.py:268
  44.7 0.0 collective-permute-done.6.g1_ref
  44.7 0.0 slice-done
  44.7 0.0 slice-done.1
  44.7 1.8 %project.1 = (f32[3,16,2048]{2,1,0:T(8,128)S(1)}, f32[3,16,2048]{2,1,0:T(8,128)S(1)}, bf16[2,3,16,2048]{3,2,1,0:T(8,128)(2,1)S(1)}) custom-call(bf16[3,16,2048]{2,1,0:T(8,128)(2,1)S(1)} %merge.1.own_ref, bf16[3,16,2048]{2,1,0:T(8,128)(2,1)S(1)} %collective-permute-done.6.g1_ref, bf16[3,16,2048]{2,1,0:T(8,128)(2,1)S(1)} %collective-permute-done.7.g2_ref, ...), custom_call_target="tpu_custom_call" | custom-call | flops 1610612736 | bytes 8388608 | tf_op jit(solution)/shard_map/project/pallas_call | solution.py:397
  46.6 0.1 collective-permute-start.9
  46.6 1.7 %collective-permute-done.9.got_ref = bf16[2,3,16,2048]{3,2,1,0:T(8,128)(2,1)S(1)} collective-permute-done((bf16[2,3,16,2048]{3,2,1,0:T(8,128)(2,1)S(1)}, bf16[2,3,16,2048]{3,2,1,0:T(8,128)(2,1)S(1)}, u32[]{:S(2)}, u32[]{:S(2)}) %collective-permute-start.9) | collective-permute-done | bytes 393248 | tf_op jit(solution)/shard_map/ppermute | solution.py:268
  48.4 1.5 %collective-permute-start.10 = (bf16[3,16,2048]{2,1,0:T(8,128)(2,1)S(1)}, bf16[3,16,2048]{2,1,0:T(8,128)(2,1)S(1)}, u32[]{:S(2)}, u32[]{:S(2)}) collective-permute-start(bf16[3,16,2048]{2,1,0:T(8,128)(2,1)S(1)} %add.21), channel_id=1, source_target_pairs={{0,2},{1,3},{2,0},{3,1},{4,6},{5,7},{6,4},{7,5},{8,10},{9,11},{10,... | collective-permute-start | bytes 589832 | tf_op jit(solution)/shard_map/ppermute | solution.py:268
  50.0 5.5 %collective-permute-done.10 = bf16[3,16,2048]{2,1,0:T(8,128)(2,1)S(1)} collective-permute-done((bf16[3,16,2048]{2,1,0:T(8,128)(2,1)S(1)}, bf16[3,16,2048]{2,1,0:T(8,128)(2,1)S(1)}, u32[]{:S(2)}, u32[]{:S(2)}) %collective-permute-start.10) | collective-permute-done | bytes 196640 | tf_op jit(solution)/shard_map/ppermute | solution.py:268
  55.4 0.7 %fusion.2 = bf16[16,3,2048]{2,0,1:T(8,128)(2,1)} fusion(bf16[3,16,2048]{2,1,0:T(8,128)(2,1)S(1)} %collective-permute-done.10, f32[3,16,2048]{2,1,0:T(8,128)S(1)} %get-tuple-element.28, bf16[2,3,16,2048]{3,2,1,0:T(8,128)(2,1)S(1)} %collective-permute-done.9.got_ref), kind=kLoop, calls=%fused_computation.3 | loop fusion | flops 491520 | bytes 983040 | tf_op jit(solution)/shard_map/transpose | solution.py:423
  (2 shorter events, 0.0 us)
Async XLA Ops:
  1.2 9.4 %collective-permute-start = (bf16[3,8,2048]{2,1,0:T(8,128)(2,1)S(1)}, bf16[3,8,2048]{2,1,0:T(8,128)(2,1)S(1)}, u32[]{:S(2)}, u32[]{:S(2)}) collective-permute-start(bf16[3,8,2048]{2,1,0:T(8,128)(2,1)S(1)} %get-tuple-element.23), channel_id=1, source_target_pairs={{0,4},{4,0},{8,12},{12,8},{1,5},{5,1},{9,13},{13,9},{2,6},{6,2},{1... | collective-permute-start | bytes 294920 | tf_op jit(solution)/shard_map/ppermute | solution.py:268
  4.3 10.5 %collective-permute-start.2 = (bf16[3,8,2048]{2,1,0:T(8,128)(2,1)S(1)}, bf16[3,8,2048]{2,1,0:T(8,128)(2,1)S(1)}, u32[]{:S(2)}, u32[]{:S(2)}) collective-permute-start(bf16[3,8,2048]{2,1,0:T(8,128)(2,1)S(1)} %get-tuple-element.24), channel_id=1, source_target_pairs={{0,8},{4,12},{8,0},{12,4},{1,9},{5,13},{9,1},{13,5},{2,10},{6,14},... | collective-permute-start | bytes 294920 | tf_op jit(solution)/shard_map/ppermute | solution.py:268
  6.9 11.3 %collective-permute-start.4 = (bf16[3,8,2048]{2,1,0:T(8,128)(2,1)S(1)}, bf16[3,8,2048]{2,1,0:T(8,128)(2,1)S(1)}, u32[]{:S(2)}, u32[]{:S(2)}) collective-permute-start(bf16[3,8,2048]{2,1,0:T(8,128)(2,1)S(1)} %get-tuple-element.25), channel_id=1, source_target_pairs={{0,12},{4,8},{8,4},{12,0},{1,13},{5,9},{9,5},{13,1},{2,14},{6,10},... | collective-permute-start | bytes 294920 | tf_op jit(solution)/shard_map/ppermute | solution.py:268
  6.9 37.8 %slice-start = ((s8[8388608]{0:T(1024)(128)(4,1)}), s8[4194304]{0:T(1024)(128)(4,1)S(1)}, s32[]{:S(2)}) async-start(s8[8388608]{0:T(1024)(128)(4,1)} %bitcast.13), calls=%async_computation | async-start | bytes 8388608
  6.9 37.8 %slice-start.1 = ((s8[8388608]{0:T(1024)(128)(4,1)}), s8[4194304]{0:T(1024)(128)(4,1)S(1)}, s32[]{:S(2)}) async-start(s8[8388608]{0:T(1024)(128)(4,1)} %bitcast.13), calls=%async_computation.1 | async-start | bytes 8388608
  12.1 9.8 %collective-permute-start.1 = (bf16[3,8,2176]{2,1,0:T(8,128)(2,1)S(1)}, bf16[3,8,2176]{2,1,0:T(8,128)(2,1)S(1)}, u32[]{:S(2)}, u32[]{:S(2)}) collective-permute-start(bf16[3,8,2176]{2,1,0:T(8,128)(2,1)S(1)} %prompt.5), channel_id=1, source_target_pairs={{0,4},{4,0},{8,12},{12,8},{1,5},{5,1},{9,13},{13,9},{2,6},{6,2},{1... | collective-permute-start | bytes 313352 | tf_op jit(solution)/shard_map/ppermute | solution.py:268
  16.3 8.5 %collective-permute-start.3 = (bf16[3,8,2176]{2,1,0:T(8,128)(2,1)S(1)}, bf16[3,8,2176]{2,1,0:T(8,128)(2,1)S(1)}, u32[]{:S(2)}, u32[]{:S(2)}) collective-permute-start(bf16[3,8,2176]{2,1,0:T(8,128)(2,1)S(1)} %prompt.6), channel_id=1, source_target_pairs={{0,8},{4,12},{8,0},{12,4},{1,9},{5,13},{9,1},{13,5},{2,10},{6,14},... | collective-permute-start | bytes 313352 | tf_op jit(solution)/shard_map/ppermute | solution.py:268
  19.7 6.6 %collective-permute-start.5 = (bf16[3,8,2176]{2,1,0:T(8,128)(2,1)S(1)}, bf16[3,8,2176]{2,1,0:T(8,128)(2,1)S(1)}, u32[]{:S(2)}, u32[]{:S(2)}) collective-permute-start(bf16[3,8,2176]{2,1,0:T(8,128)(2,1)S(1)} %prompt.7), channel_id=1, source_target_pairs={{0,12},{4,8},{8,4},{12,0},{1,13},{5,9},{9,5},{13,1},{2,14},{6,10},... | collective-permute-start | bytes 313352 | tf_op jit(solution)/shard_map/ppermute | solution.py:268
  26.8 9.6 %collective-permute-start.8 = (bf16[3,16,2048]{2,1,0:T(8,128)(2,1)S(1)}, bf16[3,16,2048]{2,1,0:T(8,128)(2,1)S(1)}, u32[]{:S(2)}, u32[]{:S(2)}) collective-permute-start(bf16[3,16,2048]{2,1,0:T(8,128)(2,1)S(1)} %merge.1.own_ref), channel_id=1, source_target_pairs={{0,12},{4,8},{8,4},{12,0},{1,13},{5,9},{9,5},{13,1},{2,14},{6,10},... | collective-permute-start | bytes 589832 | tf_op jit(solution)/shard_map/ppermute | solution.py:268
  28.6 16.1 %collective-permute-start.7 = (bf16[3,16,2048]{2,1,0:T(8,128)(2,1)S(1)}, bf16[3,16,2048]{2,1,0:T(8,128)(2,1)S(1)}, u32[]{:S(2)}, u32[]{:S(2)}) collective-permute-start(bf16[3,16,2048]{2,1,0:T(8,128)(2,1)S(1)} %merge.1.own_ref), channel_id=1, source_target_pairs={{0,8},{4,12},{8,0},{12,4},{1,9},{5,13},{9,1},{13,5},{2,10},{6,14},... | collective-permute-start | bytes 589832 | tf_op jit(solution)/shard_map/ppermute | solution.py:268
  29.6 15.1 %collective-permute-start.6 = (bf16[3,16,2048]{2,1,0:T(8,128)(2,1)S(1)}, bf16[3,16,2048]{2,1,0:T(8,128)(2,1)S(1)}, u32[]{:S(2)}, u32[]{:S(2)}) collective-permute-start(bf16[3,16,2048]{2,1,0:T(8,128)(2,1)S(1)} %merge.1.own_ref), channel_id=1, source_target_pairs={{0,4},{4,0},{8,12},{12,8},{1,5},{5,1},{9,13},{13,9},{2,6},{6,2},{1... | collective-permute-start | bytes 589832 | tf_op jit(solution)/shard_map/ppermute | solution.py:268
  46.6 1.8 %collective-permute-start.9 = (bf16[2,3,16,2048]{3,2,1,0:T(8,128)(2,1)S(1)}, bf16[2,3,16,2048]{3,2,1,0:T(8,128)(2,1)S(1)}, u32[]{:S(2)}, u32[]{:S(2)}) collective-permute-start(bf16[2,3,16,2048]{3,2,1,0:T(8,128)(2,1)S(1)} %get-tuple-element.29), channel_id=1, source_target_pairs={{0,1},{1,0},{2,3},{3,2},{4,5},{5,4},{6,7},{7,6},{8,9},{9,8},{10,11... | collective-permute-start | bytes 1179656 | tf_op jit(solution)/shard_map/ppermute | solution.py:268
  48.4 7.0 %collective-permute-start.10 = (bf16[3,16,2048]{2,1,0:T(8,128)(2,1)S(1)}, bf16[3,16,2048]{2,1,0:T(8,128)(2,1)S(1)}, u32[]{:S(2)}, u32[]{:S(2)}) collective-permute-start(bf16[3,16,2048]{2,1,0:T(8,128)(2,1)S(1)} %add.21), channel_id=1, source_target_pairs={{0,2},{1,3},{2,0},{3,1},{4,6},{5,7},{6,4},{7,5},{8,10},{9,11},{10,... | collective-permute-start | bytes 589832 | tf_op jit(solution)/shard_map/ppermute | solution.py:268
